TPU v7x, 8 devices: a whole 2x2x1 slice. The times are simulated.
8 devices in a mesh: dp: 2 (over z, y), tp: 4 (over x, core).
Axes of the slice: x: 2, y: 2, z: 1, core: 2. Of those that a mesh axis runs over, the one named last changes fastest.
Arguments:
- resid_in: bfloat16 [512, 4096], P('dp'), parts along dimension 0
- positions: int32 [512], P('dp'), parts along dimension 0
- k_cache: bfloat16 [512, 256, 8, 128], P('dp', None, 'tp'), parts along dimension 0
- v_cache: bfloat16 [512, 256, 8, 128], P('dp', None, 'tp'), parts along dimension 0
- gain_attn: bfloat16 [4096], replicated
- w_query: bfloat16 [4096, 4096], P(None, 'tp')
- w_key: bfloat16 [4096, 1024], P(None, 'tp')
- w_value: bfloat16 [4096, 1024], P(None, 'tp')
- w_out: bfloat16 [4096, 4096], P('tp')
- gain_mlp: bfloat16 [4096], replicated
- w_gate: bfloat16 [4096, 14336], P(None, 'tp')
- w_up: bfloat16 [4096, 14336], P(None, 'tp')
- w_down: bfloat16 [14336, 4096], P('tp')
Outputs:
- output 1: bfloat16 [512, 4096], P('dp'), parts along dimension 0
- output 2: bfloat16 [512, 256, 8, 128], P('dp', None, 'tp'), parts along dimension 0
- output 3: bfloat16 [512, 256, 8, 128], P('dp', None, 'tp'), parts along dimension 0
There are 2 independent parts. A program takes and returns all parts, laid end to end along the dimension named above; an argument that names none is the same for every part.
All inputs are finite; a program needn't handle non-finite values.
Results may differ from a plain program's by a relative error of at most 0.0103738.
Values sent between devices are 32-bit elements.
A program may use at most 1 GiB of HBM per device.

v0:
```python
import math
import jax
import jax.numpy as jnp
from jax import lax
from jax.sharding import PartitionSpec as P

EPS = 1e-5
ROPE_THETA = 500000.0
ROPE_FACTOR = 8.0
LOW_FACTOR = 1.0
HIGH_FACTOR = 4.0
ORIG_CTX = 8192.0


def rms_norm(rows_in, gain):
    rows_f = rows_in.astype(jnp.float32)
    mean_sq = jnp.mean(rows_f * rows_f, axis=-1, keepdims=True)
    return (rows_f * lax.rsqrt(mean_sq + EPS) * gain.astype(jnp.float32)).astype(jnp.bfloat16)


def rope_tables(positions, head_dim):
    half_dim = head_dim // 2
    exponents = jnp.arange(half_dim, dtype=jnp.float32) * (2.0 / head_dim)
    inv_freq = 1.0 / jnp.power(ROPE_THETA, exponents)
    wavelen = (2.0 * math.pi) / inv_freq
    smooth = (ORIG_CTX / wavelen - LOW_FACTOR) / (HIGH_FACTOR - LOW_FACTOR)
    blended = (1.0 - smooth) * inv_freq / ROPE_FACTOR + smooth * inv_freq
    inv_freq = jnp.where(wavelen < ORIG_CTX / HIGH_FACTOR, inv_freq,
                         jnp.where(wavelen > ORIG_CTX / LOW_FACTOR, inv_freq / ROPE_FACTOR, blended))
    angles = positions.astype(jnp.float32)[:, None] * inv_freq[None, :]
    return jnp.cos(angles), jnp.sin(angles)


def apply_rope(vectors, cos_t, sin_t):
    half_dim = vectors.shape[-1] // 2
    lower_half = vectors[..., :half_dim]
    upper_half = vectors[..., half_dim:]
    cos_b = cos_t[:, None, :]
    sin_b = sin_t[:, None, :]
    return jnp.concatenate([lower_half * cos_b - upper_half * sin_b,
                            upper_half * cos_b + lower_half * sin_b], axis=-1)


def attention_block(resid_in, positions, k_cache, v_cache, gain_attn, w_query, w_key, w_value):
    n_seqs = resid_in.shape[0]
    cache_len = k_cache.shape[1]
    kv_heads = k_cache.shape[2]
    head_dim = k_cache.shape[3]
    group_size = w_query.shape[1] // (kv_heads * head_dim)
    normed = rms_norm(resid_in, gain_attn)
    queries = jnp.dot(normed, w_query, preferred_element_type=jnp.float32).astype(jnp.bfloat16)
    key_new = jnp.dot(normed, w_key, preferred_element_type=jnp.float32).astype(jnp.bfloat16)
    value_new = jnp.dot(normed, w_value, preferred_element_type=jnp.float32).astype(jnp.bfloat16)
    cos_t, sin_t = rope_tables(positions, head_dim)
    queries = apply_rope(queries.reshape(n_seqs, kv_heads * group_size, head_dim).astype(jnp.float32), cos_t, sin_t)
    queries = queries.astype(jnp.bfloat16).reshape(n_seqs, kv_heads, group_size, head_dim)
    key_new = apply_rope(key_new.reshape(n_seqs, kv_heads, head_dim).astype(jnp.float32), cos_t, sin_t)
    key_new = key_new.astype(jnp.bfloat16)
    value_new = value_new.reshape(n_seqs, kv_heads, head_dim)
    slot_iota = lax.broadcasted_iota(jnp.int32, (n_seqs, cache_len), 1)
    slot_hit = (slot_iota == positions[:, None])[:, :, None, None]
    k_full = jnp.where(slot_hit, key_new[:, None], k_cache)
    v_full = jnp.where(slot_hit, value_new[:, None], v_cache)
    scores = jnp.einsum('bkgd,bskd->bkgs', queries, k_full, preferred_element_type=jnp.float32)
    scores = scores * (1.0 / math.sqrt(head_dim))
    valid = (slot_iota <= positions[:, None])[:, None, None, :]
    scores = jnp.where(valid, scores, -jnp.inf)
    attn_prob = jax.nn.softmax(scores, axis=-1).astype(jnp.bfloat16)
    attn_out = jnp.einsum('bkgs,bskd->bkgd', attn_prob, v_full, preferred_element_type=jnp.float32)
    attn_out = attn_out.astype(jnp.bfloat16).reshape(n_seqs, kv_heads * group_size * head_dim)
    return attn_out, k_full, v_full


def gated_hidden(normed, w_gate, w_up):
    gate_proj = jnp.dot(normed, w_gate, preferred_element_type=jnp.float32).astype(jnp.bfloat16)
    up_proj = jnp.dot(normed, w_up, preferred_element_type=jnp.float32).astype(jnp.bfloat16)
    return (jax.nn.silu(gate_proj.astype(jnp.float32)) * up_proj.astype(jnp.float32)).astype(jnp.bfloat16)


def solution(mesh):
    def layer_local(resid_in, positions, k_cache, v_cache, gain_attn, w_query, w_key, w_value,
                    w_out, gain_mlp, w_gate, w_up, w_down):
        attn_out, k_full, v_full = attention_block(resid_in, positions, k_cache, v_cache,
                                                   gain_attn, w_query, w_key, w_value)
        y_part = jnp.dot(attn_out, w_out, preferred_element_type=jnp.float32)
        y_sum = lax.psum(y_part, 'tp')
        resid_mid = (resid_in.astype(jnp.float32) + y_sum).astype(jnp.bfloat16)
        hidden = gated_hidden(rms_norm(resid_mid, gain_mlp), w_gate, w_up)
        z_part = jnp.dot(hidden, w_down, preferred_element_type=jnp.float32)
        z_sum = lax.psum(z_part, 'tp')
        resid_out = (resid_mid.astype(jnp.float32) + z_sum).astype(jnp.bfloat16)
        return resid_out, k_full, v_full

    row_spec = P('dp', None)
    cache_spec = P('dp', None, 'tp', None)
    col_spec = P(None, 'tp')
    split_rows = P('tp', None)
    return jax.shard_map(layer_local, mesh=mesh,
                         in_specs=(row_spec, P('dp'), cache_spec, cache_spec, P(), col_spec, col_spec,
                                   col_spec, split_rows, P(), col_spec, col_spec, split_rows),
                         out_specs=(row_spec, cache_spec, cache_spec), check_vma=False)
```

profile of v0, /device:TPU:0, one launch (start us, length us, event | category | flops | bytes accessed | tf_op | source)
XLA Modules:
  0.0 380.8 jit_solution(17533136628816456729)
XLA Ops:
  7.2 0.0 copy-start
  7.2 0.0 all-reduce.3.cloned.1.call-start
  7.2 0.8 convert_element_type.84
  8.1 0.8 iota_compare_fusion.1
  8.9 2.1 fusion.9
  11.0 0.7 convert_element_type.79
  11.7 0.3 multiply_cosine_fusion
  12.0 0.1 copy.22
  12.1 0.1 copy.23
  12.2 2.7 convolution_convert_fusion.4
  15.1 0.1 copy.24
  15.2 3.5 convolution_convert_fusion.3
  18.7 0.1 copy.26
  18.8 5.7 %fusion.23 = f32[32,8,8,128]{3,1,2,0:T(8,128)S(1)} fusion(bf16[4096,1024]{1,0:T(8,128)(2,1)} %param.18, bf16[256,4096]{1,0:T(8,128)(2,1)S(1)} %copy-done.2, f32[4096]{0:T(1024)S(1)} %convert_element_type.79, f32[256]{0:T(256)S(1)} %add_rsqrt_fusion.1), kind=kOutput, calls=%fused_computation.37 | convolution fusion | flops 2152202240 | bytes 11551744 | tf_op jit(solution)/shard_map/dot_general | solution.py:51
  24.6 0.2 copy.28
  24.8 0.4 subtract_convert_fusion
  25.2 90.7 %broadcast_select_fusion.1 = (bf16[256,256,2,128]{3,2,1,0:T(2,128)(2,1)}, bf16[256,256,2,128]{3,2,1,0:T(2,128)(2,1)}) fusion(bf16[256,256,2,128]{3,2,1,0:T(2,128)(2,1)} %param.15, pred[256,256]{1,0:T(8,128)(4,1)S(1)} %get-tuple-element.14, bf16[256,2,128]{2,1,0:T(2,128)(2,1)S(1)} %copy.24, bf16[256,256,2,128]{3,2,1,0:T(2,128)(2,1)} %param.16, ...), kind=kLoop, calls=%fused_computation.2 | loop fusion | flops 33554432 | bytes 134545408 | tf_op jit(solution)/shard_map/jit(_where)/select_n | solution.py:62
  116.0 16.8 %fusion.45 = (f32[256,2,4]{2,1,0:T(2,128)S(1)}, f32[256,2,4,256]{3,2,1,0:T(4,128)}) fusion(pred[256,256]{1,0:T(8,128)(4,1)S(1)} %get-tuple-element.13, bf16[256,256,2,128]{3,2,1,0:T(2,128)(2,1)} %get-tuple-element.9, bf16[256,2,4,64]{3,2,1,0:T(4,128)(2,1)S(1)} %bitcast.18, bf16[256,2,4,64]{3,2,1,0:T(4,128)(2,1)S(1)} %bitcast.17), kind=kOutput, calls=%fused_computation.65 | convolution fusion | flops 137363712 | bytes 36249600 | tf_op jit(solution)/shard_map/sub | solution.py:68
  132.8 15.7 %fusion.24 = bf16[256,2,4,128]{3,2,1,0:T(4,128)(2,1)S(1)} fusion(bf16[256,256,2,128]{3,2,1,0:T(2,128)(2,1)} %get-tuple-element.10, f32[256,2,4,256]{3,2,1,0:T(4,128)} %get-tuple-element.16, f32[256,2,4]{2,1,0:T(2,128)S(1)} %get-tuple-element.15), kind=kOutput, calls=%fused_computation.38 | convolution fusion | flops 135528448 | bytes 36184064 | tf_op jit(solution)/shard_map/bkgs,bskd->bkgd/dot_general | solution.py:69
  148.5 0.4 reshape.155
  148.8 7.7 %fusion.54 = f32[256,4096]{1,0:T(8,128)} fusion(bf16[256,1024]{1,0:T(8,128)(2,1)S(1)} %reshape.155, bf16[1024,4096]{1,0:T(8,128)(2,1)} %param.21), kind=kOutput, calls=%fused_computation.66 | convolution fusion | flops 2147483648 | bytes 13107200 | tf_op jit(solution)/shard_map/dot_general | solution.py:85
  156.5 0.0 all-reduce.3.cloned.1.call-update
  156.6 0.3 all-reduce.5.cloned.1.call-start
  156.8 0.4 copy-done.5
  157.2 82.0 %all-reduce.3.cloned.1.call-done = f32[256,4096]{1,0:T(8,128)} async-done(((f32[256,4096]{1,0:T(8,128)}), f32[256,4096]{1,0:T(8,128)}) %all-reduce.3.cloned.1.call-update) | async-done | bytes 4194320 | tf_op jit(solution)/shard_map/psum | solution.py:86
  239.3 3.0 fusion.13
  242.3 1.3 copy-done.4
  243.6 15.2 %fusion.8 = f32[256,3584]{1,0:T(8,128)} fusion(bf16[4096,3584]{1,0:T(8,128)(2,1)} %param.23, bf16[256,4096]{1,0:T(8,128)(2,1)S(1)} %get-tuple-element.4, f32[4096]{0:T(1024)S(1)} %convert_element_type.93, f32[256]{0:T(256)S(1)} %add_rsqrt_fusion), kind=kOutput, calls=%fused_computation.18 | convolution fusion | flops 7522222080 | bytes 35144704 | tf_op jit(solution)/shard_map/dot_general | solution.py:75
  258.9 30.3 %fusion.17 = f32[256,4096]{1,0:T(8,128)} fusion(bf16[3584,4096]{1,0:T(8,128)(2,1)} %param.25, bf16[4096,3584]{1,0:T(8,128)(2,1)} %param.24, f32[256,3584]{1,0:T(8,128)} %fusion.8, bf16[256,4096]{1,0:T(8,128)(2,1)} %copy-done.4, f32[4096]{0:T(1024)S(1)} %convert_element_type.93, f32[256]{0:T(256)S(1)} %add_rsqrt_fusion), kind=kOutput, calls=%fused_computation.27 | convolution fusion | flops 15043919872 | bytes 68699136 | tf_op jit(solution)/shard_map/dot_general | solution.py:89
  289.2 0.0 all-reduce.5.cloned.1.call-update
  289.2 80.0 %all-reduce.5.cloned.1.call-done = f32[256,4096]{1,0:T(8,128)} async-done(((f32[256,4096]{1,0:T(8,128)}), f32[256,4096]{1,0:T(8,128)}) %all-reduce.5.cloned.1.call-update) | async-done | bytes 4194320 | tf_op jit(solution)/shard_map/psum | solution.py:90
  369.2 4.7 %fusion.16 = bf16[256,4096]{1,0:T(8,128)(2,1)} fusion(f32[256,4096]{1,0:T(8,128)} %all-reduce.5.cloned.1.call-done, bf16[256,4096]{1,0:T(8,128)(2,1)} %copy-done.4), kind=kLoop, calls=%fused_computation.26 | loop fusion | flops 3145728 | bytes 8388608 | tf_op jit(solution)/shard_map/convert_element_type | solution.py:91
  (16 shorter events, 0.1 us)
Async XLA Ops:
  7.2 5.0 %copy-start = (bf16[4096,256]{1,0:T(8,128)(2,1)S(1)}, bf16[4096,256]{1,0:T(8,128)(2,1)}, u32[]{:S(2)}) copy-start(bf16[4096,256]{1,0:T(8,128)(2,1)} %param.19) | copy-start | bytes 6291460
  7.2 232.1 %all-reduce.3.cloned.1.call-start = ((), (), s32[]{:S(2)}) async-start(), calls=%async_computation | async-start | bytes 8388608 | tf_op jit(solution)/shard_map/psum | solution.py:86
  15.0 3.8 %copy-start.2 = (bf16[256,4096]{1,0:T(8,128)(2,1)S(1)}, bf16[256,4096]{1,0:T(8,128)(2,1)}, u32[]{:S(2)}) copy-start(bf16[256,4096]{1,0:T(8,128)(2,1)} %param.13) | copy-start | bytes 6291460
  156.5 0.7 copy-start.5
  156.5 82.7 %copy-start.3 = (bf16[256,4096]{1,0:T(8,128)(2,1)S(1)}, bf16[256,4096]{1,0:T(8,128)(2,1)}, u32[]{:S(2)}) copy-start(bf16[256,4096]{1,0:T(8,128)(2,1)} %param.13) | copy-start | bytes 6291460
  156.6 212.7 %all-reduce.5.cloned.1.call-start = ((), (), s32[]{:S(2)}) async-start(), calls=%async_computation.1 | async-start | bytes 8388608 | tf_op jit(solution)/shard_map/psum | solution.py:90
  242.3 1.3 copy-start.4
  289.2 84.8 %copy-start.1 = (bf16[4096,256]{1,0:T(8,128)(2,1)S(1)}, bf16[4096,256]{1,0:T(8,128)(2,1)}, u32[]{:S(2)}) copy-start(bf16[4096,256]{1,0:T(8,128)(2,1)} %param.19) | copy-start | bytes 6291460
Sparse Core Ops, SparseCore 0:
  156.7 82.5 all-reduce.2
  289.3 79.8 all-reduce.4
where the time goes:
time: 381 us
  waiting for transfers between devices  162 us (43%)
  other arithmetic  104 us (27%)
  matrix products  97.7 us (26%)
  between operations  14.2 us (4%)
    select_n x1, other arithmetic, attention_block(): k_full = jnp.where(slot_hit, key_new[:, None], k_cache)  90.7 us
    psum x1, waiting for transfers between devices, layer_local(): y_sum = lax.psum(y_part, 'tp')  82 us
    psum x1, waiting for transfers between devices, layer_local(): z_sum = lax.psum(z_part, 'tp')  80 us
    dot_general x1, matrix products, layer_local(): z_part = jnp.dot(hidden, w_down, preferred_element_type=jnp.float32)  30.3 us
    sub x1, matrix products, attention_block(): attn_prob = jax.nn.softmax(scores, axis=-1).astype(jnp.bfloat16)  16.8 us
    dot_general x1, matrix products, attention_block(): jnp.einsum('bkgs,bskd->bkgd', attn_prob, v_full, preferred_element_type=j...  15.7 us
    dot_general x1, matrix products, gated_hidden(): jnp.dot(normed, w_gate, preferred_element_type=jnp.float32)  15.2 us
    dot_general x1, matrix products, layer_local(): y_part = jnp.dot(attn_out, w_out, preferred_element_type=jnp.float32)  7.69 us
  transfers between devices with their start and end apart: 2, of which 2 were waited for; matrix products, arithmetic and copies ran while one was open for 0% of the time, Pallas kernels for 0%

commit v1 on v0

v1 whole, which is shorter than its diff:
```python
import functools
import math
import jax
import jax.numpy as jnp
from jax import lax
from jax.experimental import pallas as pl
from jax.experimental.pallas import tpu as pltpu
from jax.sharding import PartitionSpec as P

EPS = 1e-5
ROPE_THETA = 500000.0
ROPE_FACTOR = 8.0
LOW_FACTOR = 1.0
HIGH_FACTOR = 4.0
ORIG_CTX = 8192.0

F32 = jnp.float32
BF16 = jnp.bfloat16
SEQS = 256
SLOTS = 256
WIDTH = 4096
HALF = WIDTH // 2
HD = 128
QH = 8
KVH = 2
FFN = 3584
VMEM_ALL = 67043328

ROWS = 32
CHUNKS = SEQS // ROWS
BLK = 8
BLKS = ROWS // BLK
KVSLOTS = 3
TN = 512
NT = HALF // TN
WSLOTS = 5
GT = FFN // TN
N_TILES = 2 * GT + 2 * NT


def rope_tables(positions, head_dim):
    half_dim = head_dim // 2
    exponents = jnp.arange(half_dim, dtype=jnp.float32) * (2.0 / head_dim)
    inv_freq = 1.0 / jnp.power(ROPE_THETA, exponents)
    wavelen = (2.0 * math.pi) / inv_freq
    smooth = (ORIG_CTX / wavelen - LOW_FACTOR) / (HIGH_FACTOR - LOW_FACTOR)
    blended = (1.0 - smooth) * inv_freq / ROPE_FACTOR + smooth * inv_freq
    inv_freq = jnp.where(wavelen < ORIG_CTX / HIGH_FACTOR, inv_freq,
                         jnp.where(wavelen > ORIG_CTX / LOW_FACTOR, inv_freq / ROPE_FACTOR, blended))
    angles = positions.astype(jnp.float32)[:, None] * inv_freq[None, :]
    return jnp.cos(angles), jnp.sin(angles)


def norm_rows(rows_f, gain_f):
    mean_sq = jnp.mean(rows_f * rows_f, axis=-1, keepdims=True)
    return (rows_f * lax.rsqrt(mean_sq + EPS) * gain_f).astype(BF16)


def qkv_kernel(gain_ref, cos_ref, sin_ref, x_hbm, wq_hbm, wk_hbm, wv_hbm,
               q_ref, kx_ref, vx_ref, kn_ref, vn_ref, x_ref, h_ref, w_ref, x_sem, w_sem):
    cols = 256
    nq = QH * HD // cols
    load_x = pltpu.make_async_copy(x_hbm, x_ref, x_sem)
    load_x.start()
    loads = [pltpu.make_async_copy(wq_hbm.at[:, i * cols:(i + 1) * cols], w_ref.at[i], w_sem.at[i])
             for i in range(nq)]
    loads.append(pltpu.make_async_copy(wk_hbm, w_ref.at[nq], w_sem.at[nq]))
    loads.append(pltpu.make_async_copy(wv_hbm, w_ref.at[nq + 1], w_sem.at[nq + 1]))
    for load in loads:
        load.start()
    load_x.wait()
    gain_f = gain_ref[...].astype(F32)

    def norm_step(i, _):
        rows = pl.ds(pl.multiple_of(i * 16, 16), 16)
        h_ref[rows, :] = norm_rows(x_ref[rows, :].astype(F32), gain_f)
        return 0

    lax.fori_loop(0, SEQS // 16, norm_step, 0)

    def rotate(v):
        return (v * cos_ref[...] + pltpu.roll(v, HD // 2, 1) * sin_ref[...]).astype(BF16).astype(F32)

    for i, load in enumerate(loads):
        load.wait()
        prod = jnp.dot(h_ref[...], w_ref[i], preferred_element_type=F32).astype(BF16).astype(F32)
        for j in range(2):
            head = prod[:, j * HD:(j + 1) * HD]
            if i < nq:
                q_ref[:, 2 * i + j, :] = rotate(head)
            elif i == nq:
                head = rotate(head)
                kn_ref[:, j * HD:(j + 1) * HD] = head.astype(BF16)
                for g in range(QH // KVH):
                    kx_ref[:, j * (QH // KVH) + g, :] = head
            else:
                vn_ref[:, j * HD:(j + 1) * HD] = head.astype(BF16)
                for g in range(QH // KVH):
                    vx_ref[:, j * (QH // KVH) + g, :] = head


def qkv(resid_in, gain, cos_t, sin_t, w_query, w_key, w_value):
    vmem = pl.BlockSpec(memory_space=pltpu.VMEM)
    hbm = pl.BlockSpec(memory_space=pl.ANY)
    shape = jax.ShapeDtypeStruct
    return pl.pallas_call(
        qkv_kernel,
        name="qkv",
        out_shape=(shape((SEQS, QH, HD), F32), shape((SEQS, QH, HD), F32), shape((SEQS, QH, HD), F32),
                   shape((SEQS, KVH * HD), BF16), shape((SEQS, KVH * HD), BF16)),
        in_specs=[vmem] * 3 + [hbm] * 4,
        out_specs=(vmem,) * 5,
        scratch_shapes=[pltpu.VMEM((SEQS, WIDTH), BF16), pltpu.VMEM((SEQS, WIDTH), BF16),
                        pltpu.VMEM((6, WIDTH, 256), BF16), pltpu.SemaphoreType.DMA, pltpu.SemaphoreType.DMA((6,))],
        compiler_params=pltpu.CompilerParams(vmem_limit_bytes=VMEM_ALL),
        cost_estimate=pl.CostEstimate(flops=2 * SEQS * WIDTH * 1536, bytes_accessed=16 * 2**20, transcendentals=0),
    )(gain, cos_t, sin_t, resid_in, w_query, w_key, w_value)


CBLK = 16
CSLOTS = 12


def cache_kernel(pos_ref, kn_ref, vn_ref, k_hbm, v_hbm, after_hbm, k_out, v_out, buf, in_sem, out_sem):
    steps = [(src, dst, new, i) for i in range(SEQS // CBLK)
             for src, dst, new in ((k_hbm, k_out, kn_ref), (v_hbm, v_out, vn_ref))]
    n = len(steps)
    ahead = CSLOTS // 2

    def load(s):
        src, _, _, i = steps[s]
        return pltpu.make_async_copy(src.at[pl.ds(i * CBLK, CBLK)], buf.at[s % CSLOTS], in_sem.at[s % CSLOTS])

    def save(s):
        _, dst, _, i = steps[s]
        return pltpu.make_async_copy(buf.at[s % CSLOTS], dst.at[pl.ds(i * CBLK, CBLK)], out_sem.at[s % CSLOTS])

    for s in range(ahead):
        load(s).start()
    for s in range(n):
        if s + ahead < n:
            if s + ahead >= CSLOTS:
                save(s + ahead - CSLOTS).wait()
            load(s + ahead).start()
        load(s).wait()
        _, _, new, i = steps[s]

        def patch(j, _, new=new, i=i, s=s):
            row = i * CBLK + j
            buf[s % CSLOTS, j, pos_ref[row]] = new[row]
            return 0

        lax.fori_loop(0, CBLK, patch, 0)
        save(s).start()
    for s in range(n - CSLOTS, n):
        save(s).wait()


def write_caches(positions, kn, vn, k_cache, v_cache, after):
    vmem = pl.BlockSpec(memory_space=pltpu.VMEM)
    hbm = pl.BlockSpec(memory_space=pl.ANY)
    cache = jax.ShapeDtypeStruct(k_cache.shape, BF16)
    return pl.pallas_call(
        cache_kernel,
        name="write_caches",
        out_shape=(cache, cache),
        in_specs=[pl.BlockSpec(memory_space=pltpu.SMEM), vmem, vmem, hbm, hbm, hbm],
        out_specs=(hbm, hbm),
        scratch_shapes=[pltpu.VMEM((CSLOTS, CBLK, SLOTS, KVH, HD), BF16),
                        pltpu.SemaphoreType.DMA((CSLOTS,)), pltpu.SemaphoreType.DMA((CSLOTS,))],
        compiler_params=pltpu.CompilerParams(vmem_limit_bytes=56 * 2**20),
        cost_estimate=pl.CostEstimate(flops=2 * 10**10, bytes_accessed=128 * 2**20, transcendentals=0),
    )(positions, kn, vn, k_cache, v_cache, after)


def layer_kernel(pos_ref, q_ref, kx_ref, vx_ref, res_ref, gain_ref, k_hbm, v_hbm, wo_hbm, wg_hbm, wu_hbm, wd_hbm,
                 x1_ref, z_ref, kbuf, vbuf, wo, o3, o2, ybuf, rb1, sb, rb2, tb, h2, act, gbuf, wbuf,
                 k_sem, v_sem, wo_sem, w_sem, s1, r1, s2, r2, s3, r3, s4, r4):
    tp = lax.axis_index("tp")
    mine = lax.rem(tp, 2)
    other = 1 - mine
    partner = tp + 1 - 2 * mine
    peer = lax.rem(tp + 2, 4)

    def load_kv(g):
        slot = lax.rem(g, KVSLOTS)
        seqs = pl.ds(g * BLK, BLK)
        return (pltpu.make_async_copy(k_hbm.at[seqs], kbuf.at[slot], k_sem.at[slot]),
                pltpu.make_async_copy(v_hbm.at[seqs], vbuf.at[slot], v_sem.at[slot]))

    for g in range(KVSLOTS):
        for copy in load_kv(g):
            copy.start()

    barrier = pltpu.get_barrier_semaphore()
    for device in (partner, peer):
        pl.semaphore_signal(barrier, inc=1, device_id={"tp": device}, device_id_type=pl.DeviceIdType.MESH)
    pl.semaphore_wait(barrier, 2)

    load_wo = [pltpu.make_async_copy(wo_hbm.at[:, pl.ds(i * HALF, HALF)], wo.at[i], wo_sem.at[i]) for i in range(2)]
    for copy in load_wo:
        copy.start()

    def remote(src, dst, send, recv, device):
        return pltpu.make_async_remote_copy(src_ref=src, dst_ref=dst, send_sem=send, recv_sem=recv,
                                            device_id={"tp": device}, device_id_type=pl.DeviceIdType.MESH)

    def rows_of(c):
        return pl.ds(pl.multiple_of(c * ROWS, ROWS), ROWS)

    def send1(c):
        return remote(ybuf.at[other, :, rows_of(c)], rb1.at[:, rows_of(c)], s1.at[c], r1.at[c], partner)

    def send2(c):
        return remote(sb.at[:, rows_of(c)], rb2.at[:, rows_of(c)], s2.at[c], r2.at[c], peer)

    def send3(c):
        return remote(tb.at[mine, :, rows_of(c)], tb.at[mine, :, rows_of(c)], s3.at[c], r3.at[c], partner)

    def recv3(c):
        return remote(tb.at[other, :, rows_of(c)], tb.at[other, :, rows_of(c)], s3.at[c], r3.at[c], partner)

    def load_gate(t, slot):
        cols = pl.ds(pl.multiple_of(t * TN, TN), TN)
        return pltpu.make_async_copy(wg_hbm.at[:, cols], wbuf.at[slot], w_sem.at[slot])

    def load_up(t, slot):
        cols = pl.ds(pl.multiple_of(t * TN, TN), TN)
        return pltpu.make_async_copy(wu_hbm.at[:, cols], wbuf.at[slot], w_sem.at[slot])

    def load_down(t, slot):
        far = (t < NT).astype(jnp.int32)
        half = far * other + (1 - far) * mine
        start = half * HALF + (t - (1 - far) * NT) * TN
        cols = pl.ds(pl.multiple_of(start, TN), TN)
        return pltpu.make_async_copy(wd_hbm.at[:, cols], wbuf.at[slot, pl.ds(0, FFN)], w_sem.at[slot])

    def start_tile(i):
        slot = lax.rem(i, WSLOTS)
        odd = lax.rem(i, 2)

        @pl.when((i < 2 * GT) & (odd == 0))
        def _():
            load_gate(i // 2, slot).start()

        @pl.when((i < 2 * GT) & (odd == 1))
        def _():
            load_up(i // 2, slot).start()

        @pl.when((i >= 2 * GT) & (i < N_TILES))
        def _():
            load_down(i - 2 * GT, slot).start()

    col = lax.broadcasted_iota(jnp.int32, (QH, KVH * SLOTS), 1)
    row_head = lax.broadcasted_iota(jnp.int32, (QH, KVH * SLOTS), 0) // (QH // KVH)
    col_slot = jnp.where(lax.rem(col, KVH) == row_head, col // KVH, SLOTS)
    scale = 1.0 / math.sqrt(HD)

    def attend(g, base):
        slot = lax.rem(g, KVSLOTS)
        for copy in load_kv(g):
            copy.wait()
        qs = [q_ref[g * BLK + i] for i in range(BLK)]
        score = [lax.dot_general(qs[i].astype(BF16), kbuf[slot, i], (((1,), (1,)), ((), ())),
                                 preferred_element_type=F32) for i in range(BLK)]
        new = [jnp.sum(qs[i] * kx_ref[g * BLK + i].astype(F32), axis=1, keepdims=True) * scale for i in range(BLK)]
        score = [jnp.where(col_slot < pos_ref[g * BLK + i], score[i] * scale, -jnp.inf) for i in range(BLK)]
        top = [jnp.maximum(jnp.max(score[i], axis=1, keepdims=True), new[i]) for i in range(BLK)]
        e = [jnp.exp(score[i] - top[i]) for i in range(BLK)]
        e_new = [jnp.exp(new[i] - top[i]) for i in range(BLK)]
        inv = [1.0 / (jnp.sum(e[i], axis=1, keepdims=True) + e_new[i]) for i in range(BLK)]
        for i in range(BLK):
            prob = (e[i] * inv[i]).astype(BF16)
            prob_new = (e_new[i] * inv[i]).astype(BF16).astype(F32)
            out = jnp.dot(prob, vbuf[slot, i], preferred_element_type=F32)
            out = out + prob_new * vx_ref[g * BLK + i].astype(F32)
            o3[base + i] = out.astype(BF16).astype(F32)

        @pl.when(g + KVSLOTS < SEQS // BLK)
        def _():
            for copy in load_kv(g + KVSLOTS):
                copy.start()

    def project(c, half):
        for n in range(NT):
            ybuf[half, n, rows_of(c), :] = jnp.dot(o2[...], wo[half, :, n * TN:(n + 1) * TN],
                                                   preferred_element_type=F32)

    def stage2(c):
        send1(c).wait_recv()
        sb[:, rows_of(c)] = ybuf[mine, :, rows_of(c)] + rb1[:, rows_of(c)]
        send2(c).start()

    def stage3(c):
        send2(c).wait_recv()
        tb[mine, :, rows_of(c)] = sb[:, rows_of(c)] + rb2[:, rows_of(c)]
        send3(c).start()

    def stage4(c):
        recv3(c).wait_recv()
        gain_f = gain_ref[...].astype(F32)

        def body(i, _):
            rows = pl.ds(pl.multiple_of(c * ROWS + i * 16, 16), 16)
            total = jnp.zeros((16, 1), F32)
            for half in range(2):
                for n in range(NT):
                    cols = slice(half * HALF + n * TN, half * HALF + (n + 1) * TN)
                    x1 = (res_ref[rows, cols].astype(F32) + tb[half, n, rows, :]).astype(BF16)
                    x1_ref[rows, cols] = x1
                    x1_f = x1.astype(F32)
                    total = total + jnp.sum(x1_f * x1_f, axis=1, keepdims=True)
            inv = lax.rsqrt(total * (1.0 / WIDTH) + EPS)
            for n in range(2 * NT):
                cols = slice(n * TN, (n + 1) * TN)
                h2[rows, cols] = (x1_ref[rows, cols].astype(F32) * inv * gain_f[:, cols]).astype(BF16)
            return 0

        lax.fori_loop(0, ROWS // 16, body, 0)

    def chunk(c, _):
        def block(j, _):
            attend(c * BLKS + j, j * BLK)

            @pl.when((j == 0) & (c >= 1))
            def _():
                stage2(c - 1)

            return 0

        lax.fori_loop(0, BLKS, block, 0)
        for j in range(QH):
            o2[:, j * HD:(j + 1) * HD] = o3[:, j, :].astype(BF16)

        @pl.when(c == 0)
        def _():
            for copy in load_wo:
                copy.wait()

        project(c, other)
        send1(c).start()
        project(c, mine)

        @pl.when(c >= CHUNKS - WSLOTS)
        def _():
            start_tile(c - (CHUNKS - WSLOTS))

        @pl.when(c >= 3)
        def _():
            stage3(c - 3)

        @pl.when(c >= 4)
        def _():
            stage4(c - 4)

        return 0

    lax.fori_loop(0, CHUNKS, chunk, 0)
    stage2(CHUNKS - 1)
    stage4(CHUNKS - 4)

    def tail(c, _):
        stage3(c)
        return 0

    def tail4(c, _):
        stage4(c)
        return 0

    lax.fori_loop(CHUNKS - 3, CHUNKS, tail, 0)
    lax.fori_loop(CHUNKS - 3, CHUNKS, tail4, 0)

    def sent(c, _):
        send1(c).wait_send()
        send2(c).wait_send()
        send3(c).wait_send()
        return 0

    lax.fori_loop(0, CHUNKS, sent, 0)

    def mm(lhs_ref, slot, depth, n):
        return jnp.dot(lhs_ref[...], wbuf[slot, 0:depth, n * 256:(n + 1) * 256], preferred_element_type=F32)

    def gate_up(t, _):
        slot = lax.rem(2 * t, WSLOTS)
        load_gate(t, slot).wait()
        for n in range(TN // 256):
            gbuf[:, n * 256:(n + 1) * 256] = mm(h2, slot, WIDTH, n).astype(BF16)
        start_tile(2 * t + WSLOTS)
        slot = lax.rem(2 * t + 1, WSLOTS)
        load_up(t, slot).wait()
        for n in range(TN // 256):
            up = mm(h2, slot, WIDTH, n).astype(BF16).astype(F32)
            gate = gbuf[:, n * 256:(n + 1) * 256].astype(F32)
            act[:, pl.ds(pl.multiple_of(t * TN + n * 256, 256), 256)] = (jax.nn.silu(gate) * up).astype(BF16)
        start_tile(2 * t + 1 + WSLOTS)
        return 0

    lax.fori_loop(0, GT, gate_up, 0)

    def send4(t):
        return remote(ybuf.at[other, t], rb1.at[t], s4.at[t], r4.at[t], partner)

    def down_far(t, _):
        i = 2 * GT + t
        slot = lax.rem(i, WSLOTS)
        load_down(t, slot).wait()
        for n in range(TN // 256):
            ybuf[other, t, :, n * 256:(n + 1) * 256] = mm(act, slot, FFN, n)
        send4(t).start()
        start_tile(i + WSLOTS)
        return 0

    lax.fori_loop(0, NT, down_far, 0)

    def down_near(t, _):
        i = 2 * GT + NT + t
        slot = lax.rem(i, WSLOTS)
        load_down(NT + t, slot).wait()
        send4(t).wait_recv()
        for n in range(TN // 256):
            z_ref[t, :, n * 256:(n + 1) * 256] = mm(act, slot, FFN, n) + rb1[t, :, n * 256:(n + 1) * 256]
        start_tile(i + WSLOTS)
        return 0

    lax.fori_loop(0, NT, down_near, 0)

    def sent4(t, _):
        send4(t).wait_send()
        return 0

    lax.fori_loop(0, NT, sent4, 0)


def layer(positions, q, kx, vx, resid_in, gain, k_rows, v_rows, w_out, w_gate, w_up, w_down):
    vmem = pl.BlockSpec(memory_space=pltpu.VMEM)
    hbm = pl.BlockSpec(memory_space=pl.ANY)
    dma = pltpu.SemaphoreType.DMA
    return pl.pallas_call(
        layer_kernel,
        name="layer",
        out_shape=(jax.ShapeDtypeStruct((SEQS, WIDTH), BF16), jax.ShapeDtypeStruct((NT, SEQS, TN), F32)),
        in_specs=[pl.BlockSpec(memory_space=pltpu.SMEM)] + [vmem] * 5 + [hbm] * 6,
        out_specs=(vmem, vmem),
        scratch_shapes=[
            pltpu.VMEM((KVSLOTS, BLK, KVH * SLOTS, HD), BF16), pltpu.VMEM((KVSLOTS, BLK, KVH * SLOTS, HD), BF16),
            pltpu.VMEM((2, QH * HD, HALF), BF16),
            pltpu.VMEM((ROWS, QH, HD), F32), pltpu.VMEM((ROWS, QH * HD), BF16),
            pltpu.VMEM((2, NT, SEQS, TN), F32), pltpu.VMEM((NT, SEQS, TN), F32), pltpu.VMEM((NT, SEQS, TN), F32),
            pltpu.VMEM((NT, SEQS, TN), F32), pltpu.VMEM((2, NT, SEQS, TN), F32),
            pltpu.VMEM((SEQS, WIDTH), BF16), pltpu.VMEM((SEQS, FFN), BF16), pltpu.VMEM((SEQS, TN), BF16),
            pltpu.VMEM((WSLOTS, WIDTH, TN), BF16),
            dma((KVSLOTS,)), dma((KVSLOTS,)), dma((2,)), dma((WSLOTS,)),
            dma((CHUNKS,)), dma((CHUNKS,)), dma((CHUNKS,)), dma((CHUNKS,)), dma((CHUNKS,)), dma((CHUNKS,)),
            dma((NT,)), dma((NT,))],
        compiler_params=pltpu.CompilerParams(collective_id=0, has_side_effects=True, vmem_limit_bytes=VMEM_ALL),
        cost_estimate=pl.CostEstimate(flops=3 * 10**10, bytes_accessed=180 * 2**20, transcendentals=0),
    )(positions, q, kx, vx, resid_in, gain, k_rows, v_rows, w_out, w_gate, w_up, w_down)


def final_kernel(z_ref, zr_ref, x1_ref, out_ref, tb, send_sem, recv_sem):
    tp = lax.axis_index("tp")
    mine = lax.rem(tp, 2)
    other = 1 - mine
    partner = tp + 1 - 2 * mine
    barrier = pltpu.get_barrier_semaphore()
    pl.semaphore_signal(barrier, inc=1, device_id={"tp": partner}, device_id_type=pl.DeviceIdType.MESH)
    pl.semaphore_wait(barrier, 1)

    def copy(half, t):
        return pltpu.make_async_remote_copy(src_ref=tb.at[half, t], dst_ref=tb.at[half, t], send_sem=send_sem.at[t],
                                            recv_sem=recv_sem.at[t], device_id={"tp": partner},
                                            device_id_type=pl.DeviceIdType.MESH)

    def add(half, t):
        cols = pl.ds(pl.multiple_of(half * HALF + t * TN, TN), TN)
        out_ref[:, cols] = (x1_ref[:, cols].astype(F32) + tb[half, t]).astype(BF16)

    for t in range(NT):
        tb[mine, t] = z_ref[t] + zr_ref[t]
        copy(mine, t).start()
    for t in range(NT):
        add(mine, t)
    for t in range(NT):
        copy(other, t).wait_recv()
        add(other, t)
    for t in range(NT):
        copy(mine, t).wait_send()


def finish(z, z_peer, x1):
    vmem = pl.BlockSpec(memory_space=pltpu.VMEM)
    return pl.pallas_call(
        final_kernel,
        name="finish",
        out_shape=jax.ShapeDtypeStruct((SEQS, WIDTH), BF16),
        in_specs=[vmem] * 3,
        out_specs=vmem,
        scratch_shapes=[pltpu.VMEM((2, NT, SEQS, TN), F32), pltpu.SemaphoreType.DMA((NT,)),
                        pltpu.SemaphoreType.DMA((NT,))],
        compiler_params=pltpu.CompilerParams(collective_id=1, has_side_effects=True, vmem_limit_bytes=24 * 2**20),
        cost_estimate=pl.CostEstimate(flops=2 * 10**8, bytes_accessed=10 * 2**20, transcendentals=0),
    )(z, z_peer, x1)


def solution(mesh):
    def layer_local(resid_in, positions, k_cache, v_cache, gain_attn, w_query, w_key, w_value,
                    w_out, gain_mlp, w_gate, w_up, w_down):
        cos_t, sin_t = rope_tables(positions, HD)
        cos_t = jnp.concatenate([cos_t, cos_t], axis=1)
        sin_t = jnp.concatenate([-sin_t, sin_t], axis=1)
        q, kx, vx, kn, vn = qkv(resid_in, gain_attn.reshape(1, WIDTH), cos_t, sin_t, w_query, w_key, w_value)
        k_rows = k_cache.reshape(SEQS, SLOTS * KVH, HD)
        v_rows = v_cache.reshape(SEQS, SLOTS * KVH, HD)
        x1, z = layer(positions, q, kx, vx, resid_in, gain_mlp.reshape(1, WIDTH), k_rows, v_rows,
                      w_out, w_gate, w_up, w_down)
        z_peer = lax.ppermute(z, 'tp', [(0, 2), (1, 3), (2, 0), (3, 1)])
        k_full, v_full = write_caches(positions, kn.reshape(SEQS, KVH, HD), vn.reshape(SEQS, KVH, HD),
                                      k_cache, v_cache, z)
        resid_out = finish(z, z_peer, x1)
        return resid_out, k_full, v_full

    row_spec = P('dp', None)
    cache_spec = P('dp', None, 'tp', None)
    col_spec = P(None, 'tp')
    split_rows = P('tp', None)
    return jax.shard_map(layer_local, mesh=mesh,
                         in_specs=(row_spec, P('dp'), cache_spec, cache_spec, P(), col_spec, col_spec,
                                   col_spec, split_rows, P(), col_spec, col_spec, split_rows),
                         out_specs=(row_spec, cache_spec, cache_spec), check_vma=False)
```

time: 381 us -> 170 us (0.45)
  waiting for transfers between devices: 162 us -> 0.01 us
  Pallas kernels: 0 us -> 160 us
  other arithmetic: 104 us -> 2.08 us
  matrix products: 97.7 us -> 0 us
  between operations: 14.2 us -> 0.7 us
  local copies, waits for them, and re-layouts: 2.72 us -> 7.12 us
    psum x2 -> x0, waiting for transfers between devices: 162 us -> none  [the longest x1 82 us: layer_local(): y_sum = lax.psum(y_part, 'tp')]
    pallas_call x0 -> x4, Pallas kernels: none -> 160 us  [the longest x1 91.1 us: layer(): pl.pallas_call(layer_kernel, name='layer', out_shape=(jax.ShapeDtypeStruc...]
    select_n x1 -> x0, other arithmetic: 90.7 us -> none  [attention_block(): k_full = jnp.where(slot_hit, key_new[:, None], k_cache)]
    dot_general x7 -> x0, matrix products: 80.9 us -> none  [the longest x1 30.3 us: layer_local(): z_part = jnp.dot(hidden, w_down, preferred_element_type=jnp.float32)]
    sub x1 -> x0, matrix products: 16.8 us -> none  [attention_block(): attn_prob = jax.nn.softmax(scores, axis=-1).astype(jnp.bfloat16)]
    convert_element_type x4 -> x0, other arithmetic: 5.48 us -> none  [the longest x1 4.75 us: layer_local(): resid_out = (resid_mid.astype(jnp.float32) + z_sum).astype(jnp.bfloat16)]
    reshape x1 -> x4, local copies, waits for them, and re-layouts: 0.37 us -> 5.79 us  [the longest x1 1.59 us: layer_local(): kn.reshape(SEQS, KVH, HD)]
    reduce_sum x2 -> x0, other arithmetic: 5.1 us -> none  [rms_norm(): mean_sq = jnp.mean(rows_f * rows_f, axis=-1, keepdims=True)]
  transfers between devices with their start and end apart: 2 -> 1, of which waited for: 2 -> 0; matrix products, arithmetic and copies ran while one was open for 0% -> 2% of each run, Pallas kernels for 0% -> 27%
where the time goes in v1:
time: 170 us
  Pallas kernels  160 us (94%)
  local copies, waits for them, and re-layouts  7.12 us (4%)
  other arithmetic  2.08 us (1%)
    pallas_call x1, Pallas kernels, layer(): pl.pallas_call(layer_kernel, name='layer', out_shape=(jax.ShapeDtypeStruc...  91.1 us
    pallas_call x1, Pallas kernels, write_caches(): pl.pallas_call(cache_kernel, name='write_caches', out_shape=(cache, cache...  45.9 us
    pallas_call x1, Pallas kernels, qkv(): pl.pallas_call(qkv_kernel, name='qkv', out_shape=(shape((SEQS, QH, HD), F...  18.3 us
    pallas_call x1, Pallas kernels, finish(): pl.pallas_call(final_kernel, name='finish', out_shape=jax.ShapeDtypeStruc...  4.53 us
  transfers between devices with their start and end apart: 1, of which 0 were waited for; matrix products, arithmetic and copies ran while one was open for 2% of the time, Pallas kernels for 27%

profile of v1, /device:TPU:0, one launch (start us, length us, event | category | flops | bytes accessed | tf_op | source)
XLA Modules:
  0.0 169.9 jit_solution(12498131044960751496)
XLA Ops:
  0.7 0.7 convert_element_type.3
  1.3 1.3 reshape.47.gain_ref
  2.6 1.3 reshape.48.gain_ref
  3.9 0.5 fusion
  4.5 0.8 pad_maximum_fusion
  5.3 18.3 %qkv.1 = (f32[256,8,128]{2,1,0:T(8,128)}, f32[256,8,128]{2,1,0:T(8,128)}, f32[256,8,128]{2,1,0:T(8,128)}, bf16[256,256]{1,0:T(8,128)(2,1)}, bf16[256,256]{1,0:T(8,128)(2,1)}) custom-call(bf16[1,4096]{1,0:T(2,128)(2,1)} %reshape.47.gain_ref, f32[256,128]{1,0:T(8,128)} %get-tuple-element.24.cos_ref, f32[256,128]{1,0:T(8,128)} %get-tuple-element.25.sin_ref, ...), custom_call_target="tpu_custom_call" | custom-call | flops 3221225472 | bytes 16777216 | tf_op jit(solution)/shard_map/qkv/pallas_call | solution.py:106
  23.6 91.1 %layer.1 = (bf16[256,4096]{1,0:T(8,128)(2,1)}, f32[4,256,512]{2,1,0:T(8,128)}) custom-call(s32[256]{0:T(256)} %pos_ref.3, f32[256,8,128]{2,1,0:T(8,128)} %get-tuple-element.12.q_ref, f32[256,8,128]{2,1,0:T(8,128)} %get-tuple-element.13.kx_ref, f32[256,8,128]{2,1,0:T(8,128)} %get-tuple-element.14.vx_ref, bf16[256,4096]{1,0:T(8,128)(2,1)} %res_ref.1, ...), custom_call_target="tpu_custom_call" | custom-call | flops 30000001024 | bytes 188743680 | tf_op jit(solution)/shard_map/layer/pallas_call | solution.py:439
  114.7 0.2 collective-permute-start
  114.9 1.6 reshape.51.kn_ref
  116.5 1.6 reshape.52.vn_ref
  118.1 0.0 copy-start
  118.1 0.0 copy-start.1
  118.1 45.9 %write_caches.1 = (bf16[256,256,2,128]{3,2,1,0:T(2,128)(2,1)}, bf16[256,256,2,128]{3,2,1,0:T(2,128)(2,1)}) custom-call(s32[256]{0:T(256)} %pos_ref.3, bf16[256,2,128]{2,1,0:T(2,128)(2,1)} %reshape.51.kn_ref, bf16[256,2,128]{2,1,0:T(2,128)(2,1)} %reshape.52.vn_ref, bf16[256,256,2,128]{3,2,1,0:T(2,128)(2,1)} %k_hbm.1, bf16[256,256,2,128]{3,2,1,0:T(2,128)(2,1)} %v_hbm.1, ...), custom_call_target="tpu_custom_call" | custom-call | flops 20000000000 | bytes 134217728 | tf_op jit(solution)/shard_map/write_caches/pallas_call | solution.py:163
  164.0 0.0 collective-permute-done.zr_ref
  164.0 0.0 copy-done
  164.0 0.0 copy-done.1
  164.0 4.5 %finish.1 = bf16[256,4096]{1,0:T(8,128)(2,1)S(1)} custom-call(f32[4,256,512]{2,1,0:T(8,128)S(1)} %copy-done.1, f32[4,256,512]{2,1,0:T(8,128)S(1)} %collective-permute-done.zr_ref, bf16[256,4096]{1,0:T(8,128)(2,1)S(1)} %copy-done), custom_call_target="tpu_custom_call" | custom-call | flops 200000000 | bytes 10485760 | tf_op jit(solution)/shard_map/finish/pallas_call | solution.py:493
  168.6 1.3 copy.17
  (1 shorter events, 0.0 us)
Async XLA Ops:
  114.7 49.3 %collective-permute-start = (f32[4,256,512]{2,1,0:T(8,128)}, f32[4,256,512]{2,1,0:T(8,128)S(1)}, u32[]{:S(2)}, u32[]{:S(2)}) collective-permute-start(f32[4,256,512]{2,1,0:T(8,128)} %get-tuple-element.15.z_ref.after_hbm), channel_id=1, source_target_pairs={{0,2},{1,3},{2,0},{3,1},{4,6},{5,7},{6,4},{7,5}} | collective-permute-start | bytes 6291464 | tf_op jit(solution)/shard_map/ppermute | solution.py:517
  118.1 45.9 %copy-start = (bf16[256,4096]{1,0:T(8,128)(2,1)S(1)}, bf16[256,4096]{1,0:T(8,128)(2,1)}, u32[]{:S(2)}) copy-start(bf16[256,4096]{1,0:T(8,128)(2,1)} %get-tuple-element.16.x1_ref) | copy-start | bytes 6291460
  118.1 45.9 %copy-start.1 = (f32[4,256,512]{2,1,0:T(8,128)S(1)}, f32[4,256,512]{2,1,0:T(8,128)}, u32[]{:S(2)}) copy-start(f32[4,256,512]{2,1,0:T(8,128)} %get-tuple-element.15.z_ref.after_hbm) | copy-start | bytes 6291460

commit v2 on v1

v2 whole, which is shorter than its diff:
```python
import functools
import math
import jax
import jax.numpy as jnp
from jax import lax
from jax.experimental import pallas as pl
from jax.experimental.pallas import tpu as pltpu
from jax.sharding import PartitionSpec as P

EPS = 1e-5
ROPE_THETA = 500000.0
ROPE_FACTOR = 8.0
LOW_FACTOR = 1.0
HIGH_FACTOR = 4.0
ORIG_CTX = 8192.0

F32 = jnp.float32
BF16 = jnp.bfloat16
SEQS = 256
SLOTS = 256
WIDTH = 4096
HALF = WIDTH // 2
HD = 128
QH = 8
KVH = 2
FFN = 3584
VMEM_ALL = 67043328

ROWS = 32
CHUNKS = SEQS // ROWS
BLK = 8
BLKS = ROWS // BLK
KVSLOTS = 3
TN = 512
NT = HALF // TN
WSLOTS = 8
GT = FFN // TN
N_TILES = 2 * GT + 2 * NT


def rope_tables(positions, head_dim):
    half_dim = head_dim // 2
    lane = jnp.arange(head_dim)
    exponents = (lane % half_dim).astype(jnp.float32) * (2.0 / head_dim)
    inv_freq = 1.0 / jnp.power(ROPE_THETA, exponents)
    wavelen = (2.0 * math.pi) / inv_freq
    smooth = (ORIG_CTX / wavelen - LOW_FACTOR) / (HIGH_FACTOR - LOW_FACTOR)
    blended = (1.0 - smooth) * inv_freq / ROPE_FACTOR + smooth * inv_freq
    inv_freq = jnp.where(wavelen < ORIG_CTX / HIGH_FACTOR, inv_freq,
                         jnp.where(wavelen > ORIG_CTX / LOW_FACTOR, inv_freq / ROPE_FACTOR, blended))
    angles = positions[:, None].astype(jnp.float32) * inv_freq[None, :]
    sign = jnp.where(lane < half_dim, -1.0, 1.0).astype(jnp.float32)
    return jnp.cos(angles), jnp.sin(angles) * sign[None, :]


CBLK = 8
CSLOTS = 24


def cache_kernel(pos_ref, kn_ref, vn_ref, k_hbm, v_hbm, after_hbm, k_out, v_out, buf, in_sem, out_sem):
    steps = [(src, dst, new, i) for i in range(SEQS // CBLK)
             for src, dst, new in ((k_hbm, k_out, kn_ref), (v_hbm, v_out, vn_ref))]
    n = len(steps)
    ahead = CSLOTS // 2

    def load(s):
        src, _, _, i = steps[s]
        return pltpu.make_async_copy(src.at[pl.ds(i * CBLK, CBLK)], buf.at[s % CSLOTS], in_sem.at[s % CSLOTS])

    def save(s):
        _, dst, _, i = steps[s]
        return pltpu.make_async_copy(buf.at[s % CSLOTS], dst.at[pl.ds(i * CBLK, CBLK)], out_sem.at[s % CSLOTS])

    for s in range(ahead):
        load(s).start()
    for s in range(n):
        if s + ahead < n:
            if s + ahead >= CSLOTS:
                save(s + ahead - CSLOTS).wait()
            load(s + ahead).start()
        load(s).wait()
        _, _, new, i = steps[s]

        def patch(j, _, new=new, i=i, s=s):
            row = i * CBLK + j
            buf[s % CSLOTS, j, pos_ref[row]] = new[row].astype(BF16)
            return 0

        lax.fori_loop(0, CBLK, patch, 0)
        save(s).start()
    for s in range(n - CSLOTS, n):
        save(s).wait()


def write_caches(positions, kn, vn, k_cache, v_cache, after):
    vmem = pl.BlockSpec(memory_space=pltpu.VMEM)
    hbm = pl.BlockSpec(memory_space=pl.ANY)
    cache = jax.ShapeDtypeStruct(k_cache.shape, BF16)
    return pl.pallas_call(
        cache_kernel,
        name="write_caches",
        out_shape=(cache, cache),
        in_specs=[pl.BlockSpec(memory_space=pltpu.SMEM), vmem, vmem, hbm, hbm, hbm],
        out_specs=(hbm, hbm),
        scratch_shapes=[pltpu.VMEM((CSLOTS, CBLK, SLOTS, KVH, HD), BF16),
                        pltpu.SemaphoreType.DMA((CSLOTS,)), pltpu.SemaphoreType.DMA((CSLOTS,))],
        compiler_params=pltpu.CompilerParams(vmem_limit_bytes=56 * 2**20),
        cost_estimate=pl.CostEstimate(flops=2 * 10**10, bytes_accessed=128 * 2**20, transcendentals=0),
    )(positions, kn, vn, k_cache, v_cache, after)


KS = 512
SLABS = WIDTH // KS
QKV = (QH + 2 * KVH) * HD


def spread_gain(gain_ref, gain_row):
    for n in range(WIDTH // 128):
        gain_row[:, n * 128:(n + 1) * 128] = jnp.broadcast_to(gain_ref[n:n + 1, :].astype(F32), (8, 128))


def attention_kernel(pos_ref, cos_ref, sin_ref, gain1_ref, gain2_ref, x_hbm, wq_hbm, wk_hbm, wv_hbm, k_hbm, v_hbm,
                     wo_hbm, x1_ref, h2, kn_ref, vn_ref, x_ref, h_ref, w_ref, acc, q_ref, kx_ref, vx_ref, gain_row,
                     kbuf, vbuf, wo, o3, o2, ybuf, rb1, sb, rb2, tb,
                     x_sem, q_sem, k_sem, v_sem, kc_sem, vc_sem, wo_sem, s1, r1, s2, r2, s3, r3):
    tp = lax.axis_index("tp")
    mine = lax.rem(tp, 2)
    other = 1 - mine
    partner = tp + 1 - 2 * mine
    peer = lax.rem(tp + 2, 4)

    load_x = pltpu.make_async_copy(x_hbm, x_ref, x_sem)
    load_x.start()

    def load_w(i):
        rows = pl.ds(i * KS, KS)
        nq = QH * HD
        return (pltpu.make_async_copy(wq_hbm.at[rows], w_ref.at[rows, pl.ds(0, nq)], q_sem.at[i]),
                pltpu.make_async_copy(wk_hbm.at[rows], w_ref.at[rows, pl.ds(nq, KVH * HD)], k_sem.at[i]),
                pltpu.make_async_copy(wv_hbm.at[rows], w_ref.at[rows, pl.ds(nq + KVH * HD, KVH * HD)], v_sem.at[i]))

    for i in range(SLABS):
        for copy in load_w(i):
            copy.start()

    def load_kv(g):
        slot = lax.rem(g, KVSLOTS)
        seqs = pl.ds(g * BLK, BLK)
        return (pltpu.make_async_copy(k_hbm.at[seqs], kbuf.at[slot], kc_sem.at[slot]),
                pltpu.make_async_copy(v_hbm.at[seqs], vbuf.at[slot], vc_sem.at[slot]))

    for g in range(2):
        for copy in load_kv(g):
            copy.start()
    load_wo = [pltpu.make_async_copy(wo_hbm.at[:, pl.ds(i * HALF, HALF)], wo.at[i], wo_sem.at[i]) for i in range(2)]
    for copy in load_wo:
        copy.start()
    for g in range(2, KVSLOTS):
        for copy in load_kv(g):
            copy.start()

    barrier = pltpu.get_barrier_semaphore()
    for device in (partner, peer):
        pl.semaphore_signal(barrier, inc=1, device_id={"tp": device}, device_id_type=pl.DeviceIdType.MESH)

    spread_gain(gain1_ref, gain_row)
    acc[...] = jnp.zeros_like(acc)
    load_x.wait()

    def norm_step(i, _):
        rows = pl.ds(pl.multiple_of(i * 16, 16), 16)
        total = jnp.zeros((16, 1), F32)
        for n in range(2 * NT):
            part = x_ref[rows, n * TN:(n + 1) * TN].astype(F32)
            total = total + jnp.sum(part * part, axis=1, keepdims=True)
        inv = lax.rsqrt(total * (1.0 / WIDTH) + EPS)
        for n in range(2 * NT):
            cols = slice(n * TN, (n + 1) * TN)
            h_ref[rows, cols] = (x_ref[rows, cols].astype(F32) * inv * gain_row[0:1, cols]).astype(BF16)
        return 0

    lax.fori_loop(0, SEQS // 16, norm_step, 0)

    def slab(i, _):
        for copy in load_w(i):
            copy.wait()
        rows = pl.ds(pl.multiple_of(i * KS, KS), KS)
        for n in range(QKV // TN):
            cols = slice(n * TN, (n + 1) * TN)
            acc[:, cols] += jnp.dot(h_ref[:, rows], w_ref[rows, cols], preferred_element_type=F32)
        return 0

    lax.fori_loop(0, SLABS, slab, 0)

    def split(r, _):
        rows = pl.ds(pl.multiple_of(r * 32, 32), 32)
        cos_r = cos_ref[rows, :]
        sin_r = sin_ref[rows, :]

        def head(j):
            return acc[rows, j * HD:(j + 1) * HD].astype(BF16).astype(F32)

        def rotate(v):
            return (v * cos_r + pltpu.roll(v, HD // 2, 1) * sin_r).astype(BF16).astype(F32)

        for j in range(QH):
            q_ref[rows, j, :] = rotate(head(j))
        group = QH // KVH
        for j in range(KVH):
            key = rotate(head(QH + j))
            value = head(QH + KVH + j)
            kn_ref[rows, j, :] = key
            vn_ref[rows, j, :] = value
            for i in range(group):
                kx_ref[rows, j * group + i, :] = key
                vx_ref[rows, j * group + i, :] = value
        return 0

    lax.fori_loop(0, SEQS // 32, split, 0)
    spread_gain(gain2_ref, gain_row)
    pl.semaphore_wait(barrier, 2)

    def remote(src, dst, send, recv, device):
        return pltpu.make_async_remote_copy(src_ref=src, dst_ref=dst, send_sem=send, recv_sem=recv,
                                            device_id={"tp": device}, device_id_type=pl.DeviceIdType.MESH)

    def rows_of(c):
        return pl.ds(pl.multiple_of(c * ROWS, ROWS), ROWS)

    def send1(c):
        return remote(ybuf.at[other, :, rows_of(c)], rb1.at[:, rows_of(c)], s1.at[c], r1.at[c], partner)

    def send2(c):
        return remote(sb.at[:, rows_of(c)], rb2.at[:, rows_of(c)], s2.at[c], r2.at[c], peer)

    def send3(c):
        return remote(tb.at[mine, :, rows_of(c)], tb.at[mine, :, rows_of(c)], s3.at[c], r3.at[c], partner)

    def recv3(c):
        return remote(tb.at[other, :, rows_of(c)], tb.at[other, :, rows_of(c)], s3.at[c], r3.at[c], partner)

    col = lax.broadcasted_iota(jnp.int32, (QH, KVH * SLOTS), 1)
    row_head = lax.broadcasted_iota(jnp.int32, (QH, KVH * SLOTS), 0) // (QH // KVH)
    col_slot = jnp.where(lax.rem(col, KVH) == row_head, col // KVH, SLOTS)
    scale = 1.0 / math.sqrt(HD)

    def attend(g, base):
        slot = lax.rem(g, KVSLOTS)
        for copy in load_kv(g):
            copy.wait()
        qs = [q_ref[g * BLK + i] for i in range(BLK)]
        score = [lax.dot_general(qs[i].astype(BF16), kbuf[slot, i], (((1,), (1,)), ((), ())),
                                 preferred_element_type=F32) for i in range(BLK)]
        new = [jnp.sum(qs[i] * kx_ref[g * BLK + i], axis=1, keepdims=True) * scale for i in range(BLK)]
        score = [jnp.where(col_slot < pos_ref[g * BLK + i], score[i] * scale, -jnp.inf) for i in range(BLK)]
        top = [jnp.maximum(jnp.max(score[i], axis=1, keepdims=True), new[i]) for i in range(BLK)]
        e = [jnp.exp(score[i] - top[i]) for i in range(BLK)]
        e_new = [jnp.exp(new[i] - top[i]) for i in range(BLK)]
        inv = [1.0 / (jnp.sum(e[i], axis=1, keepdims=True) + e_new[i]) for i in range(BLK)]
        for i in range(BLK):
            prob = (e[i] * inv[i]).astype(BF16)
            prob_new = (e_new[i] * inv[i]).astype(BF16).astype(F32)
            out = jnp.dot(prob, vbuf[slot, i], preferred_element_type=F32)
            out = out + prob_new * vx_ref[g * BLK + i]
            o3[base + i] = out.astype(BF16).astype(F32)

        @pl.when(g + KVSLOTS < SEQS // BLK)
        def _():
            for copy in load_kv(g + KVSLOTS):
                copy.start()

    def project(c, half):
        for n in range(NT):
            ybuf[half, n, rows_of(c), :] = jnp.dot(o2[...], wo[half, :, n * TN:(n + 1) * TN],
                                                   preferred_element_type=F32)

    def stage2(c):
        send1(c).wait_recv()
        sb[:, rows_of(c)] = ybuf[mine, :, rows_of(c)] + rb1[:, rows_of(c)]
        send2(c).start()

    def stage3(c):
        send2(c).wait_recv()
        tb[mine, :, rows_of(c)] = sb[:, rows_of(c)] + rb2[:, rows_of(c)]
        send3(c).start()

    def stage4(c):
        recv3(c).wait_recv()

        def body(i, _):
            rows = pl.ds(pl.multiple_of(c * ROWS + i * 16, 16), 16)
            total = jnp.zeros((16, 1), F32)
            for half in range(2):
                for n in range(NT):
                    cols = slice(half * HALF + n * TN, half * HALF + (n + 1) * TN)
                    x1 = (x_ref[rows, cols].astype(F32) + tb[half, n, rows, :]).astype(BF16)
                    x1_ref[rows, cols] = x1
                    x1_f = x1.astype(F32)
                    total = total + jnp.sum(x1_f * x1_f, axis=1, keepdims=True)
            inv = lax.rsqrt(total * (1.0 / WIDTH) + EPS)
            for n in range(2 * NT):
                cols = slice(n * TN, (n + 1) * TN)
                h2[rows, cols] = (x1_ref[rows, cols].astype(F32) * inv * gain_row[0:1, cols]).astype(BF16)
            return 0

        lax.fori_loop(0, ROWS // 16, body, 0)

    def chunk(c, _):
        def block(j, _):
            attend(c * BLKS + j, j * BLK)

            @pl.when((j == 0) & (c >= 1))
            def _():
                stage2(c - 1)

            return 0

        lax.fori_loop(0, BLKS, block, 0)
        for j in range(QH):
            o2[:, j * HD:(j + 1) * HD] = o3[:, j, :].astype(BF16)

        @pl.when(c == 0)
        def _():
            for copy in load_wo:
                copy.wait()

        project(c, other)
        send1(c).start()
        project(c, mine)

        @pl.when(c >= 3)
        def _():
            stage3(c - 3)

        @pl.when(c >= 4)
        def _():
            stage4(c - 4)

        return 0

    lax.fori_loop(0, CHUNKS, chunk, 0)
    stage2(CHUNKS - 1)
    stage4(CHUNKS - 4)

    def tail(c, _):
        @pl.when(c < CHUNKS)
        def _():
            stage3(c)

        @pl.when(c > CHUNKS - 3)
        def _():
            stage4(c - 1)

        return 0

    lax.fori_loop(CHUNKS - 3, CHUNKS + 1, tail, 0)

    def sent(c, _):
        send1(c).wait_send()
        send2(c).wait_send()
        send3(c).wait_send()
        return 0

    lax.fori_loop(0, CHUNKS, sent, 0)


def attention(positions, cos_t, sin_t, gain1, gain2, resid_in, w_query, w_key, w_value, k_rows, v_rows, w_out):
    vmem = pl.BlockSpec(memory_space=pltpu.VMEM)
    hbm = pl.BlockSpec(memory_space=pl.ANY)
    dma = pltpu.SemaphoreType.DMA
    shape = jax.ShapeDtypeStruct
    return pl.pallas_call(
        attention_kernel,
        name="attention",
        out_shape=(shape((SEQS, WIDTH), BF16), shape((SEQS, WIDTH), BF16),
                   shape((SEQS, KVH, HD), F32), shape((SEQS, KVH, HD), F32)),
        in_specs=[pl.BlockSpec(memory_space=pltpu.SMEM)] + [vmem] * 4 + [hbm] * 7,
        out_specs=(vmem,) * 4,
        scratch_shapes=[
            pltpu.VMEM((SEQS, WIDTH), BF16), pltpu.VMEM((SEQS, WIDTH), BF16), pltpu.VMEM((WIDTH, QKV), BF16),
            pltpu.VMEM((SEQS, QKV), F32),
            pltpu.VMEM((SEQS, QH, HD), F32), pltpu.VMEM((SEQS, QH, HD), F32), pltpu.VMEM((SEQS, QH, HD), F32),
            pltpu.VMEM((8, WIDTH), F32),
            pltpu.VMEM((KVSLOTS, BLK, KVH * SLOTS, HD), BF16), pltpu.VMEM((KVSLOTS, BLK, KVH * SLOTS, HD), BF16),
            pltpu.VMEM((2, QH * HD, HALF), BF16),
            pltpu.VMEM((ROWS, QH, HD), F32), pltpu.VMEM((ROWS, QH * HD), BF16),
            pltpu.VMEM((2, NT, SEQS, TN), F32), pltpu.VMEM((NT, SEQS, TN), F32), pltpu.VMEM((NT, SEQS, TN), F32),
            pltpu.VMEM((NT, SEQS, TN), F32), pltpu.VMEM((2, NT, SEQS, TN), F32),
            dma, dma((SLABS,)), dma((SLABS,)), dma((SLABS,)), dma((KVSLOTS,)), dma((KVSLOTS,)), dma((2,)),
            dma((CHUNKS,)), dma((CHUNKS,)), dma((CHUNKS,)), dma((CHUNKS,)), dma((CHUNKS,)), dma((CHUNKS,))],
        compiler_params=pltpu.CompilerParams(collective_id=0, has_side_effects=True, vmem_limit_bytes=VMEM_ALL),
        cost_estimate=pl.CostEstimate(flops=10**10, bytes_accessed=100 * 2**20, transcendentals=0),
    )(positions, cos_t, sin_t, gain1, gain2, resid_in, w_query, w_key, w_value, k_rows, v_rows, w_out)


def mlp_kernel(h2, wg_hbm, wu_hbm, wd_hbm, z_ref, act, gbuf, wbuf, zs, zr, w_sem, s4, r4):
    tp = lax.axis_index("tp")
    mine = lax.rem(tp, 2)
    other = 1 - mine
    partner = tp + 1 - 2 * mine

    def load_gate(t, slot):
        cols = pl.ds(pl.multiple_of(t * TN, TN), TN)
        return pltpu.make_async_copy(wg_hbm.at[:, cols], wbuf.at[slot], w_sem.at[slot])

    def load_up(t, slot):
        cols = pl.ds(pl.multiple_of(t * TN, TN), TN)
        return pltpu.make_async_copy(wu_hbm.at[:, cols], wbuf.at[slot], w_sem.at[slot])

    def load_down(t, slot):
        if isinstance(t, int):
            t = jnp.int32(t)
        far = (t < NT).astype(jnp.int32)
        half = far * other + (1 - far) * mine
        start = half * HALF + (t - (1 - far) * NT) * TN
        cols = pl.ds(pl.multiple_of(start, TN), TN)
        return pltpu.make_async_copy(wd_hbm.at[:, cols], wbuf.at[slot, pl.ds(0, FFN)], w_sem.at[slot])

    def start_tile(i):
        slot = lax.rem(i, WSLOTS)
        odd = lax.rem(i, 2)

        @pl.when((i < 2 * GT) & (odd == 0))
        def _():
            load_gate(i // 2, slot).start()

        @pl.when((i < 2 * GT) & (odd == 1))
        def _():
            load_up(i // 2, slot).start()

        @pl.when((i >= 2 * GT) & (i < N_TILES))
        def _():
            load_down(i - 2 * GT, slot).start()

    def first(i, _):
        start_tile(i)
        return 0

    lax.fori_loop(0, WSLOTS, first, 0)
    barrier = pltpu.get_barrier_semaphore()
    pl.semaphore_signal(barrier, inc=1, device_id={"tp": partner}, device_id_type=pl.DeviceIdType.MESH)
    pl.semaphore_wait(barrier, 1)

    def mm(lhs_ref, slot, depth, n):
        return jnp.dot(lhs_ref[...], wbuf[slot, 0:depth, n * 256:(n + 1) * 256], preferred_element_type=F32)

    def gate_up(t, _):
        slot = lax.rem(2 * t, WSLOTS)
        load_gate(t, slot).wait()
        for n in range(TN // 256):
            gbuf[:, n * 256:(n + 1) * 256] = mm(h2, slot, WIDTH, n).astype(BF16)
        start_tile(2 * t + WSLOTS)
        slot = lax.rem(2 * t + 1, WSLOTS)
        load_up(t, slot).wait()
        for n in range(TN // 256):
            up = mm(h2, slot, WIDTH, n).astype(BF16).astype(F32)
            gate = gbuf[:, n * 256:(n + 1) * 256].astype(F32)
            act[:, pl.ds(pl.multiple_of(t * TN + n * 256, 256), 256)] = (jax.nn.silu(gate) * up).astype(BF16)
        start_tile(2 * t + 1 + WSLOTS)
        return 0

    lax.fori_loop(0, GT, gate_up, 0)

    def send4(t):
        return pltpu.make_async_remote_copy(src_ref=zs.at[t], dst_ref=zr.at[t], send_sem=s4.at[t], recv_sem=r4.at[t],
                                            device_id={"tp": partner}, device_id_type=pl.DeviceIdType.MESH)

    def down_far(t, _):
        i = 2 * GT + t
        slot = lax.rem(i, WSLOTS)
        load_down(t, slot).wait()
        for n in range(TN // 256):
            zs[t, :, n * 256:(n + 1) * 256] = mm(act, slot, FFN, n)
        send4(t).start()
        start_tile(i + WSLOTS)
        return 0

    lax.fori_loop(0, NT, down_far, 0)

    def down_near(t, _):
        i = 2 * GT + NT + t
        slot = lax.rem(i, WSLOTS)
        load_down(NT + t, slot).wait()
        send4(t).wait_recv()
        for n in range(TN // 256):
            z_ref[t, :, n * 256:(n + 1) * 256] = mm(act, slot, FFN, n) + zr[t, :, n * 256:(n + 1) * 256]
        start_tile(i + WSLOTS)
        return 0

    lax.fori_loop(0, NT, down_near, 0)

    def sent4(t, _):
        send4(t).wait_send()
        return 0

    lax.fori_loop(0, NT, sent4, 0)


def mlp(h2, w_gate, w_up, w_down):
    vmem = pl.BlockSpec(memory_space=pltpu.VMEM)
    hbm = pl.BlockSpec(memory_space=pl.ANY)
    dma = pltpu.SemaphoreType.DMA
    return pl.pallas_call(
        mlp_kernel,
        name="mlp",
        out_shape=jax.ShapeDtypeStruct((NT, SEQS, TN), F32),
        in_specs=[vmem] + [hbm] * 3,
        out_specs=vmem,
        scratch_shapes=[
            pltpu.VMEM((SEQS, FFN), BF16), pltpu.VMEM((SEQS, TN), BF16), pltpu.VMEM((WSLOTS, WIDTH, TN), BF16),
            pltpu.VMEM((NT, SEQS, TN), F32), pltpu.VMEM((NT, SEQS, TN), F32),
            dma((WSLOTS,)), dma((NT,)), dma((NT,))],
        compiler_params=pltpu.CompilerParams(collective_id=2, has_side_effects=True, vmem_limit_bytes=VMEM_ALL),
        cost_estimate=pl.CostEstimate(flops=2 * 10**10, bytes_accessed=90 * 2**20, transcendentals=0),
    )(h2, w_gate, w_up, w_down)


def final_kernel(z_ref, zr_ref, x1_ref, out_ref, tb, send_sem, recv_sem):
    tp = lax.axis_index("tp")
    mine = lax.rem(tp, 2)
    other = 1 - mine
    partner = tp + 1 - 2 * mine
    barrier = pltpu.get_barrier_semaphore()
    pl.semaphore_signal(barrier, inc=1, device_id={"tp": partner}, device_id_type=pl.DeviceIdType.MESH)
    pl.semaphore_wait(barrier, 1)

    def copy(half, t):
        return pltpu.make_async_remote_copy(src_ref=tb.at[half, t], dst_ref=tb.at[half, t], send_sem=send_sem.at[t],
                                            recv_sem=recv_sem.at[t], device_id={"tp": partner},
                                            device_id_type=pl.DeviceIdType.MESH)

    def add(half, t):
        cols = pl.ds(pl.multiple_of(half * HALF + t * TN, TN), TN)
        out_ref[:, cols] = (x1_ref[:, cols].astype(F32) + tb[half, t]).astype(BF16)

    for t in range(NT):
        tb[mine, t] = z_ref[t] + zr_ref[t]
        copy(mine, t).start()
    for t in range(NT):
        add(mine, t)
    for t in range(NT):
        copy(other, t).wait_recv()
        add(other, t)
    for t in range(NT):
        copy(mine, t).wait_send()


def finish(z, z_peer, x1):
    vmem = pl.BlockSpec(memory_space=pltpu.VMEM)
    return pl.pallas_call(
        final_kernel,
        name="finish",
        out_shape=jax.ShapeDtypeStruct((SEQS, WIDTH), BF16),
        in_specs=[vmem] * 3,
        out_specs=vmem,
        scratch_shapes=[pltpu.VMEM((2, NT, SEQS, TN), F32), pltpu.SemaphoreType.DMA((NT,)),
                        pltpu.SemaphoreType.DMA((NT,))],
        compiler_params=pltpu.CompilerParams(collective_id=1, has_side_effects=True, vmem_limit_bytes=24 * 2**20),
        cost_estimate=pl.CostEstimate(flops=2 * 10**8, bytes_accessed=10 * 2**20, transcendentals=0),
    )(z, z_peer, x1)


def solution(mesh):
    def layer_local(resid_in, positions, k_cache, v_cache, gain_attn, w_query, w_key, w_value,
                    w_out, gain_mlp, w_gate, w_up, w_down):
        cos_t, sin_t = rope_tables(positions, HD)
        k_rows = k_cache.reshape(SEQS, SLOTS * KVH, HD)
        v_rows = v_cache.reshape(SEQS, SLOTS * KVH, HD)
        x1, h2, kn, vn = attention(positions, cos_t, sin_t, gain_attn.reshape(32, 128), gain_mlp.reshape(32, 128),
                                   resid_in, w_query, w_key, w_value, k_rows, v_rows, w_out)
        z = mlp(h2, w_gate, w_up, w_down)
        z_peer = lax.ppermute(z, 'tp', [(0, 2), (1, 3), (2, 0), (3, 1)])
        k_full, v_full = write_caches(positions, kn, vn, k_cache, v_cache, z)
        resid_out = finish(z, z_peer, x1)
        return resid_out, k_full, v_full

    row_spec = P('dp', None)
    cache_spec = P('dp', None, 'tp', None)
    col_spec = P(None, 'tp')
    split_rows = P('tp', None)
    return jax.shard_map(layer_local, mesh=mesh,
                         in_specs=(row_spec, P('dp'), cache_spec, cache_spec, P(), col_spec, col_spec,
                                   col_spec, split_rows, P(), col_spec, col_spec, split_rows),
                         out_specs=(row_spec, cache_spec, cache_spec), check_vma=False)
```

time: 170 us -> 165 us (0.971)
  local copies, waits for them, and re-layouts: 7.12 us -> 1.33 us
  waiting for transfers between devices: 0.01 us -> 2.58 us
  Pallas kernels: 160 us -> 158 us
    reshape x4 -> x0, local copies, waits for them, and re-layouts: 5.79 us -> none  [the longest x1 1.59 us: layer_local(): kn.reshape(SEQS, KVH, HD)]
    ppermute x1, waiting for transfers between devices: 0.01 us -> 2.58 us  [layer_local(): z_peer = lax.ppermute(z, 'tp', [(0, 2), (1, 3), (2, 0), (3, 1)])]
  transfers between devices with their start and end apart: 1 -> 1, of which waited for: 0 -> 1; matrix products, arithmetic and copies ran while one was open for 2% -> 0% of each run, Pallas kernels for 27% -> 28%
where the time goes in v2:
time: 165 us
  Pallas kernels  158 us (96%)
  waiting for transfers between devices  2.58 us (2%)
  other arithmetic  1.94 us (1%)
    pallas_call x1, Pallas kernels, attention(): pl.pallas_call(attention_kernel, name='attention', out_shape=(shape((SEQS...  76.4 us
    pallas_call x1, Pallas kernels, write_caches(): pl.pallas_call(cache_kernel, name='write_caches', out_shape=(cache, cache...  45.7 us
    pallas_call x1, Pallas kernels, mlp(): pl.pallas_call(mlp_kernel, name='mlp', out_shape=jax.ShapeDtypeStruct((NT...  31.7 us
    pallas_call x1, Pallas kernels, finish(): pl.pallas_call(final_kernel, name='finish', out_shape=jax.ShapeDtypeStruc...  4.35 us
  transfers between devices with their start and end apart: 1, of which 1 were waited for; matrix products, arithmetic and copies ran while one was open for 0% of the time, Pallas kernels for 28%

profile of v2, /device:TPU:0, one launch (start us, length us, event | category | flops | bytes accessed | tf_op | source)
XLA Modules:
  0.0 164.7 jit_solution(17245627261867614396)
XLA Ops:
  0.7 0.7 convert_element_type.11
  1.3 1.2 fusion
  2.6 76.4 %attention.1 = (bf16[256,4096]{1,0:T(8,128)(2,1)}, bf16[256,4096]{1,0:T(8,128)(2,1)}, f32[256,2,128]{2,1,0:T(2,128)}, f32[256,2,128]{2,1,0:T(2,128)}) custom-call(s32[256]{0:T(256)} %pos_ref.3, f32[256,128]{1,0:T(8,128)} %get-tuple-element.16.cos_ref, f32[256,128]{1,0:T(8,128)} %get-tuple-element.15.sin_ref, bf16[32,128]{1,0:T(8,128)(2,1)} %bitcast.6, ...), custom_call_target="tpu_custom_call" | custom-call | flops 10000000000 | bytes 104857600 | tf_op jit(solution)/shard_map/attention/pallas_call | solution.py:372
  78.9 31.7 %mlp.1.z_ref.after_hbm = f32[4,256,512]{2,1,0:T(8,128)} custom-call(bf16[256,4096]{1,0:T(8,128)(2,1)} %get-tuple-element.9.h2, bf16[4096,3584]{1,0:T(8,128)(2,1)} %wg_hbm.1, bf16[4096,3584]{1,0:T(8,128)(2,1)} %wu_hbm.1, bf16[3584,4096]{1,0:T(8,128)(2,1)} %wd_hbm.1), custom_call_target="tpu_custom_call" | custom-call | flops 20000000000 | bytes 94371840 | tf_op jit(solution)/shard_map/mlp/pallas_call | solution.py:503
  110.7 0.0 collective-permute-start
  110.7 0.0 copy-start
  110.7 0.0 copy-start.1
  110.7 45.7 %write_caches.1 = (bf16[256,256,2,128]{3,2,1,0:T(2,128)(2,1)}, bf16[256,256,2,128]{3,2,1,0:T(2,128)(2,1)}) custom-call(s32[256]{0:T(256)} %pos_ref.3, f32[256,2,128]{2,1,0:T(2,128)} %get-tuple-element.11.kn_ref, f32[256,2,128]{2,1,0:T(2,128)} %get-tuple-element.12.vn_ref, bf16[256,256,2,128]{3,2,1,0:T(2,128)(2,1)} %k_hbm.1, ...), custom_call_target="tpu_custom_call" | custom-call | flops 20000000000 | bytes 134217728 | tf_op jit(solution)/shard_map/write_caches/pallas_call | solution.py:99
  156.4 2.6 %collective-permute-done.zr_ref = f32[4,256,512]{2,1,0:T(8,128)S(1)} collective-permute-done((f32[4,256,512]{2,1,0:T(8,128)}, f32[4,256,512]{2,1,0:T(8,128)S(1)}, u32[]{:S(2)}, u32[]{:S(2)}) %collective-permute-start) | collective-permute-done | bytes 2097184 | tf_op jit(solution)/shard_map/ppermute | solution.py:572
  159.0 0.0 copy-done
  159.0 0.0 copy-done.1
  159.0 4.4 %finish.1 = bf16[256,4096]{1,0:T(8,128)(2,1)S(1)} custom-call(f32[4,256,512]{2,1,0:T(8,128)S(1)} %copy-done, f32[4,256,512]{2,1,0:T(8,128)S(1)} %collective-permute-done.zr_ref, bf16[256,4096]{1,0:T(8,128)(2,1)S(1)} %copy-done.1), custom_call_target="tpu_custom_call" | custom-call | flops 200000000 | bytes 10485760 | tf_op jit(solution)/shard_map/finish/pallas_call | solution.py:550
  163.4 1.3 copy.17
  (1 shorter events, 0.0 us)
Async XLA Ops:
  110.7 48.3 %collective-permute-start = (f32[4,256,512]{2,1,0:T(8,128)}, f32[4,256,512]{2,1,0:T(8,128)S(1)}, u32[]{:S(2)}, u32[]{:S(2)}) collective-permute-start(f32[4,256,512]{2,1,0:T(8,128)} %mlp.1.z_ref.after_hbm), channel_id=1, source_target_pairs={{0,2},{1,3},{2,0},{3,1},{4,6},{5,7},{6,4},{7,5}} | collective-permute-start | bytes 6291464 | tf_op jit(solution)/shard_map/ppermute | solution.py:572
  110.7 48.3 %copy-start = (f32[4,256,512]{2,1,0:T(8,128)S(1)}, f32[4,256,512]{2,1,0:T(8,128)}, u32[]{:S(2)}) copy-start(f32[4,256,512]{2,1,0:T(8,128)} %mlp.1.z_ref.after_hbm) | copy-start | bytes 6291460
  110.7 48.3 %copy-start.1 = (bf16[256,4096]{1,0:T(8,128)(2,1)S(1)}, bf16[256,4096]{1,0:T(8,128)(2,1)}, u32[]{:S(2)}) copy-start(bf16[256,4096]{1,0:T(8,128)(2,1)} %get-tuple-element.10.x1_ref) | copy-start | bytes 6291460

commit v3 on v2

--- a/solution.py
+++ b/solution.py
@@ -33,7 +33,7 @@
 KVSLOTS = 3
 TN = 512
 NT = HALF // TN
-WSLOTS = 8
+WSLOTS = 5
 GT = FFN // TN
 N_TILES = 2 * GT + 2 * NT
 
@@ -83,7 +83,8 @@
 
         def patch(j, _, new=new, i=i, s=s):
             row = i * CBLK + j
-            buf[s % CSLOTS, j, pos_ref[row]] = new[row].astype(BF16)
+            pair = jnp.concatenate([new[h, pl.ds(row, 1), :] for h in range(KVH)], axis=0)
+            buf[s % CSLOTS, j, pos_ref[row]] = pair.astype(BF16)
             return 0
 
         lax.fori_loop(0, CBLK, patch, 0)
@@ -111,6 +112,7 @@
 
 KS = 512
 SLABS = WIDTH // KS
+PITCH = 264
 QKV = (QH + 2 * KVH) * HD
 
 
@@ -119,10 +121,12 @@
         gain_row[:, n * 128:(n + 1) * 128] = jnp.broadcast_to(gain_ref[n:n + 1, :].astype(F32), (8, 128))
 
 
-def attention_kernel(pos_ref, cos_ref, sin_ref, gain1_ref, gain2_ref, x_hbm, wq_hbm, wk_hbm, wv_hbm, k_hbm, v_hbm,
-                     wo_hbm, x1_ref, h2, kn_ref, vn_ref, x_ref, h_ref, w_ref, acc, q_ref, kx_ref, vx_ref, gain_row,
-                     kbuf, vbuf, wo, o3, o2, ybuf, rb1, sb, rb2, tb,
-                     x_sem, q_sem, k_sem, v_sem, kc_sem, vc_sem, wo_sem, s1, r1, s2, r2, s3, r3):
+def layer_kernel(pos_hbm, cos_hbm, sin_hbm, gain1_hbm, gain2_hbm, x_hbm, wq_hbm, wk_hbm, wv_hbm, k_hbm, v_hbm,
+                 wo_hbm, wg_hbm, wu_hbm, wd_hbm, x1_hbm, z_hbm, kn_ref, vn_ref,
+                 pos_ref, cos_ref, sin_ref, gain1_ref, gain2_ref, x_ref, x1_ref, h2, q_ref, gain_row,
+                 kbuf, vbuf, wo, o3, o2, ybuf, rb1, sb, rb2, tb, act, gbuf, wbuf,
+                 small_sem, x_sem, q_sem, k_sem, v_sem, kc_sem, vc_sem, wo_sem, w_sem, x1_sem, z_sem,
+                 s1, r1, s2, r2, s3, r3, s4, r4):
     tp = lax.axis_index("tp")
     mine = lax.rem(tp, 2)
     other = 1 - mine
@@ -131,13 +135,18 @@
 
     load_x = pltpu.make_async_copy(x_hbm, x_ref, x_sem)
     load_x.start()
+    small = [pltpu.make_async_copy(src, dst, small_sem.at[i]) for i, (src, dst) in enumerate(
+        ((gain1_hbm, gain1_ref), (gain2_hbm, gain2_ref), (cos_hbm, cos_ref), (sin_hbm, sin_ref), (pos_hbm, pos_ref)))]
+    for copy in small:
+        copy.start()
 
     def load_w(i):
         rows = pl.ds(i * KS, KS)
-        nq = QH * HD
-        return (pltpu.make_async_copy(wq_hbm.at[rows], w_ref.at[rows, pl.ds(0, nq)], q_sem.at[i]),
-                pltpu.make_async_copy(wk_hbm.at[rows], w_ref.at[rows, pl.ds(nq, KVH * HD)], k_sem.at[i]),
-                pltpu.make_async_copy(wv_hbm.at[rows], w_ref.at[rows, pl.ds(nq + KVH * HD, KVH * HD)], v_sem.at[i]))
+        kv = KVH * HD
+        return (pltpu.make_async_copy(wq_hbm.at[rows, pl.ds(0, TN)], wbuf.at[0, rows], q_sem.at[0, i]),
+                pltpu.make_async_copy(wq_hbm.at[rows, pl.ds(TN, TN)], wbuf.at[1, rows], q_sem.at[1, i]),
+                pltpu.make_async_copy(wk_hbm.at[rows], wbuf.at[2, rows, pl.ds(0, kv)], k_sem.at[i]),
+                pltpu.make_async_copy(wv_hbm.at[rows], wbuf.at[2, rows, pl.ds(kv, kv)], v_sem.at[i]))
 
     for i in range(SLABS):
         for copy in load_w(i):
@@ -163,8 +172,11 @@
     for device in (partner, peer):
         pl.semaphore_signal(barrier, inc=1, device_id={"tp": device}, device_id_type=pl.DeviceIdType.MESH)
 
+    for n in range(QKV // TN):
+        ybuf[0, n] = jnp.zeros((SEQS, TN), F32)
+    for copy in small:
+        copy.wait()
     spread_gain(gain1_ref, gain_row)
-    acc[...] = jnp.zeros_like(acc)
     load_x.wait()
 
     def norm_step(i, _):
@@ -176,7 +188,7 @@
         inv = lax.rsqrt(total * (1.0 / WIDTH) + EPS)
         for n in range(2 * NT):
             cols = slice(n * TN, (n + 1) * TN)
-            h_ref[rows, cols] = (x_ref[rows, cols].astype(F32) * inv * gain_row[0:1, cols]).astype(BF16)
+            h2[rows, cols] = (x_ref[rows, cols].astype(F32) * inv * gain_row[0:1, cols]).astype(BF16)
         return 0
 
     lax.fori_loop(0, SEQS // 16, norm_step, 0)
@@ -186,8 +198,7 @@
             copy.wait()
         rows = pl.ds(pl.multiple_of(i * KS, KS), KS)
         for n in range(QKV // TN):
-            cols = slice(n * TN, (n + 1) * TN)
-            acc[:, cols] += jnp.dot(h_ref[:, rows], w_ref[rows, cols], preferred_element_type=F32)
+            ybuf[0, n] += jnp.dot(h2[:, rows], wbuf[n, rows, :], preferred_element_type=F32)
         return 0
 
     lax.fori_loop(0, SLABS, slab, 0)
@@ -198,22 +209,17 @@
         sin_r = sin_ref[rows, :]
 
         def head(j):
-            return acc[rows, j * HD:(j + 1) * HD].astype(BF16).astype(F32)
+            per = TN // HD
+            return ybuf[0, j // per, rows, (j % per) * HD:(j % per + 1) * HD].astype(BF16).astype(F32)
 
         def rotate(v):
             return (v * cos_r + pltpu.roll(v, HD // 2, 1) * sin_r).astype(BF16).astype(F32)
 
         for j in range(QH):
-            q_ref[rows, j, :] = rotate(head(j))
-        group = QH // KVH
+            q_ref[pl.ds(pl.multiple_of(j * PITCH + r * 32, 8), 32), :] = rotate(head(j))
         for j in range(KVH):
-            key = rotate(head(QH + j))
-            value = head(QH + KVH + j)
-            kn_ref[rows, j, :] = key
-            vn_ref[rows, j, :] = value
-            for i in range(group):
-                kx_ref[rows, j * group + i, :] = key
-                vx_ref[rows, j * group + i, :] = value
+            kn_ref[j, rows, :] = rotate(head(QH + j))
+            vn_ref[j, rows, :] = head(QH + KVH + j)
         return 0
 
     lax.fori_loop(0, SEQS // 32, split, 0)
@@ -238,20 +244,57 @@
 
     def recv3(c):
         return remote(tb.at[other, :, rows_of(c)], tb.at[other, :, rows_of(c)], s3.at[c], r3.at[c], partner)
+
+    def load_gate(t, slot):
+        cols = pl.ds(pl.multiple_of(t * TN, TN), TN)
+        return pltpu.make_async_copy(wg_hbm.at[:, cols], wbuf.at[slot], w_sem.at[slot])
+
+    def load_up(t, slot):
+        cols = pl.ds(pl.multiple_of(t * TN, TN), TN)
+        return pltpu.make_async_copy(wu_hbm.at[:, cols], wbuf.at[slot], w_sem.at[slot])
+
+    def load_down(t, slot):
+        if isinstance(t, int):
+            t = jnp.int32(t)
+        far = (t < NT).astype(jnp.int32)
+        half = far * other + (1 - far) * mine
+        start = half * HALF + (t - (1 - far) * NT) * TN
+        cols = pl.ds(pl.multiple_of(start, TN), TN)
+        return pltpu.make_async_copy(wd_hbm.at[:, cols], wbuf.at[slot, pl.ds(0, FFN)], w_sem.at[slot])
+
+    def start_tile(i):
+        slot = lax.rem(i, WSLOTS)
+        odd = lax.rem(i, 2)
+
+        @pl.when((i < 2 * GT) & (odd == 0))
+        def _():
+            load_gate(i // 2, slot).start()
+
+        @pl.when((i < 2 * GT) & (odd == 1))
+        def _():
+            load_up(i // 2, slot).start()
+
+        @pl.when((i >= 2 * GT) & (i < N_TILES))
+        def _():
+            load_down(i - 2 * GT, slot).start()
 
     col = lax.broadcasted_iota(jnp.int32, (QH, KVH * SLOTS), 1)
     row_head = lax.broadcasted_iota(jnp.int32, (QH, KVH * SLOTS), 0) // (QH // KVH)
     col_slot = jnp.where(lax.rem(col, KVH) == row_head, col // KVH, SLOTS)
     scale = 1.0 / math.sqrt(HD)
+    low = lax.broadcasted_iota(jnp.int32, (QH, HD), 0) < QH // KVH
+
+    def by_head(ref, b):
+        return jnp.where(low, ref[0, pl.ds(b, 1), :], ref[1, pl.ds(b, 1), :])
 
     def attend(g, base):
         slot = lax.rem(g, KVSLOTS)
         for copy in load_kv(g):
             copy.wait()
-        qs = [q_ref[g * BLK + i] for i in range(BLK)]
+        qs = [q_ref[pl.ds(g * BLK + i, QH, stride=PITCH), :] for i in range(BLK)]
         score = [lax.dot_general(qs[i].astype(BF16), kbuf[slot, i], (((1,), (1,)), ((), ())),
                                  preferred_element_type=F32) for i in range(BLK)]
-        new = [jnp.sum(qs[i] * kx_ref[g * BLK + i], axis=1, keepdims=True) * scale for i in range(BLK)]
+        new = [jnp.sum(qs[i] * by_head(kn_ref, g * BLK + i), axis=1, keepdims=True) * scale for i in range(BLK)]
         score = [jnp.where(col_slot < pos_ref[g * BLK + i], score[i] * scale, -jnp.inf) for i in range(BLK)]
         top = [jnp.maximum(jnp.max(score[i], axis=1, keepdims=True), new[i]) for i in range(BLK)]
         e = [jnp.exp(score[i] - top[i]) for i in range(BLK)]
@@ -261,7 +304,7 @@
             prob = (e[i] * inv[i]).astype(BF16)
             prob_new = (e_new[i] * inv[i]).astype(BF16).astype(F32)
             out = jnp.dot(prob, vbuf[slot, i], preferred_element_type=F32)
-            out = out + prob_new * vx_ref[g * BLK + i]
+            out = out + prob_new * by_head(vn_ref, g * BLK + i)
             o3[base + i] = out.astype(BF16).astype(F32)
 
         @pl.when(g + KVSLOTS < SEQS // BLK)
@@ -328,6 +371,10 @@
         send1(c).start()
         project(c, mine)
 
+        @pl.when(c >= CHUNKS - WSLOTS)
+        def _():
+            start_tile(c - (CHUNKS - WSLOTS))
+
         @pl.when(c >= 3)
         def _():
             stage3(c - 3)
@@ -363,83 +410,8 @@
 
     lax.fori_loop(0, CHUNKS, sent, 0)
 
-
-def attention(positions, cos_t, sin_t, gain1, gain2, resid_in, w_query, w_key, w_value, k_rows, v_rows, w_out):
-    vmem = pl.BlockSpec(memory_space=pltpu.VMEM)
-    hbm = pl.BlockSpec(memory_space=pl.ANY)
-    dma = pltpu.SemaphoreType.DMA
-    shape = jax.ShapeDtypeStruct
-    return pl.pallas_call(
-        attention_kernel,
-        name="attention",
-        out_shape=(shape((SEQS, WIDTH), BF16), shape((SEQS, WIDTH), BF16),
-                   shape((SEQS, KVH, HD), F32), shape((SEQS, KVH, HD), F32)),
-        in_specs=[pl.BlockSpec(memory_space=pltpu.SMEM)] + [vmem] * 4 + [hbm] * 7,
-        out_specs=(vmem,) * 4,
-        scratch_shapes=[
-            pltpu.VMEM((SEQS, WIDTH), BF16), pltpu.VMEM((SEQS, WIDTH), BF16), pltpu.VMEM((WIDTH, QKV), BF16),
-            pltpu.VMEM((SEQS, QKV), F32),
-            pltpu.VMEM((SEQS, QH, HD), F32), pltpu.VMEM((SEQS, QH, HD), F32), pltpu.VMEM((SEQS, QH, HD), F32),
-            pltpu.VMEM((8, WIDTH), F32),
-            pltpu.VMEM((KVSLOTS, BLK, KVH * SLOTS, HD), BF16), pltpu.VMEM((KVSLOTS, BLK, KVH * SLOTS, HD), BF16),
-            pltpu.VMEM((2, QH * HD, HALF), BF16),
-            pltpu.VMEM((ROWS, QH, HD), F32), pltpu.VMEM((ROWS, QH * HD), BF16),
-            pltpu.VMEM((2, NT, SEQS, TN), F32), pltpu.VMEM((NT, SEQS, TN), F32), pltpu.VMEM((NT, SEQS, TN), F32),
-            pltpu.VMEM((NT, SEQS, TN), F32), pltpu.VMEM((2, NT, SEQS, TN), F32),
-            dma, dma((SLABS,)), dma((SLABS,)), dma((SLABS,)), dma((KVSLOTS,)), dma((KVSLOTS,)), dma((2,)),
-            dma((CHUNKS,)), dma((CHUNKS,)), dma((CHUNKS,)), dma((CHUNKS,)), dma((CHUNKS,)), dma((CHUNKS,))],
-        compiler_params=pltpu.CompilerParams(collective_id=0, has_side_effects=True, vmem_limit_bytes=VMEM_ALL),
-        cost_estimate=pl.CostEstimate(flops=10**10, bytes_accessed=100 * 2**20, transcendentals=0),
-    )(positions, cos_t, sin_t, gain1, gain2, resid_in, w_query, w_key, w_value, k_rows, v_rows, w_out)
-
-
-def mlp_kernel(h2, wg_hbm, wu_hbm, wd_hbm, z_ref, act, gbuf, wbuf, zs, zr, w_sem, s4, r4):
-    tp = lax.axis_index("tp")
-    mine = lax.rem(tp, 2)
-    other = 1 - mine
-    partner = tp + 1 - 2 * mine
-
-    def load_gate(t, slot):
-        cols = pl.ds(pl.multiple_of(t * TN, TN), TN)
-        return pltpu.make_async_copy(wg_hbm.at[:, cols], wbuf.at[slot], w_sem.at[slot])
-
-    def load_up(t, slot):
-        cols = pl.ds(pl.multiple_of(t * TN, TN), TN)
-        return pltpu.make_async_copy(wu_hbm.at[:, cols], wbuf.at[slot], w_sem.at[slot])
-
-    def load_down(t, slot):
-        if isinstance(t, int):
-            t = jnp.int32(t)
-        far = (t < NT).astype(jnp.int32)
-        half = far * other + (1 - far) * mine
-        start = half * HALF + (t - (1 - far) * NT) * TN
-        cols = pl.ds(pl.multiple_of(start, TN), TN)
-        return pltpu.make_async_copy(wd_hbm.at[:, cols], wbuf.at[slot, pl.ds(0, FFN)], w_sem.at[slot])
-
-    def start_tile(i):
-        slot = lax.rem(i, WSLOTS)
-        odd = lax.rem(i, 2)
-
-        @pl.when((i < 2 * GT) & (odd == 0))
-        def _():
-            load_gate(i // 2, slot).start()
-
-        @pl.when((i < 2 * GT) & (odd == 1))
-        def _():
-            load_up(i // 2, slot).start()
-
-        @pl.when((i >= 2 * GT) & (i < N_TILES))
-        def _():
-            load_down(i - 2 * GT, slot).start()
-
-    def first(i, _):
-        start_tile(i)
-        return 0
-
-    lax.fori_loop(0, WSLOTS, first, 0)
-    barrier = pltpu.get_barrier_semaphore()
-    pl.semaphore_signal(barrier, inc=1, device_id={"tp": partner}, device_id_type=pl.DeviceIdType.MESH)
-    pl.semaphore_wait(barrier, 1)
+    save_x1 = pltpu.make_async_copy(x1_ref, x1_hbm, x1_sem)
+    save_x1.start()
 
     def mm(lhs_ref, slot, depth, n):
         return jnp.dot(lhs_ref[...], wbuf[slot, 0:depth, n * 256:(n + 1) * 256], preferred_element_type=F32)
@@ -462,15 +434,17 @@
     lax.fori_loop(0, GT, gate_up, 0)
 
     def send4(t):
-        return pltpu.make_async_remote_copy(src_ref=zs.at[t], dst_ref=zr.at[t], send_sem=s4.at[t], recv_sem=r4.at[t],
-                                            device_id={"tp": partner}, device_id_type=pl.DeviceIdType.MESH)
+        return remote(ybuf.at[other, t], rb1.at[t], s4.at[t], r4.at[t], partner)
+
+    def save_z(t):
+        return pltpu.make_async_copy(sb.at[t], z_hbm.at[t], z_sem.at[t])
 
     def down_far(t, _):
         i = 2 * GT + t
         slot = lax.rem(i, WSLOTS)
         load_down(t, slot).wait()
         for n in range(TN // 256):
-            zs[t, :, n * 256:(n + 1) * 256] = mm(act, slot, FFN, n)
+            ybuf[other, t, :, n * 256:(n + 1) * 256] = mm(act, slot, FFN, n)
         send4(t).start()
         start_tile(i + WSLOTS)
         return 0
@@ -483,7 +457,8 @@
         load_down(NT + t, slot).wait()
         send4(t).wait_recv()
         for n in range(TN // 256):
-            z_ref[t, :, n * 256:(n + 1) * 256] = mm(act, slot, FFN, n) + zr[t, :, n * 256:(n + 1) * 256]
+            sb[t, :, n * 256:(n + 1) * 256] = mm(act, slot, FFN, n) + rb1[t, :, n * 256:(n + 1) * 256]
+        save_z(t).start()
         start_tile(i + WSLOTS)
         return 0
 
@@ -491,28 +466,46 @@
 
     def sent4(t, _):
         send4(t).wait_send()
+        save_z(t).wait()
         return 0
 
     lax.fori_loop(0, NT, sent4, 0)
-
-
-def mlp(h2, w_gate, w_up, w_down):
+    save_x1.wait()
+
+
+def layer(positions, cos_t, sin_t, gain1, gain2, resid_in, w_query, w_key, w_value, k_rows, v_rows, w_out,
+          w_gate, w_up, w_down):
     vmem = pl.BlockSpec(memory_space=pltpu.VMEM)
     hbm = pl.BlockSpec(memory_space=pl.ANY)
     dma = pltpu.SemaphoreType.DMA
+    shape = jax.ShapeDtypeStruct
+    tile = (NT, SEQS, TN)
     return pl.pallas_call(
-        mlp_kernel,
-        name="mlp",
-        out_shape=jax.ShapeDtypeStruct((NT, SEQS, TN), F32),
-        in_specs=[vmem] + [hbm] * 3,
-        out_specs=vmem,
+        layer_kernel,
+        name="layer",
+        out_shape=(shape((SEQS, WIDTH), BF16), shape(tile, F32),
+                   shape((KVH, SEQS, HD), F32), shape((KVH, SEQS, HD), F32)),
+        in_specs=[hbm] * 15,
+        out_specs=(hbm, hbm, vmem, vmem),
         scratch_shapes=[
+            pltpu.SMEM((SEQS,), jnp.int32), pltpu.VMEM((SEQS, HD), F32), pltpu.VMEM((SEQS, HD), F32),
+            pltpu.VMEM((32, 128), BF16), pltpu.VMEM((32, 128), BF16),
+            pltpu.VMEM((SEQS, WIDTH), BF16), pltpu.VMEM((SEQS, WIDTH), BF16), pltpu.VMEM((SEQS, WIDTH), BF16),
+            pltpu.VMEM((QH * PITCH, HD), F32), pltpu.VMEM((8, WIDTH), F32),
+            pltpu.VMEM((KVSLOTS, BLK, KVH * SLOTS, HD), BF16), pltpu.VMEM((KVSLOTS, BLK, KVH * SLOTS, HD), BF16),
+            pltpu.VMEM((2, QH * HD, HALF), BF16),
+            pltpu.VMEM((ROWS, QH, HD), F32), pltpu.VMEM((ROWS, QH * HD), BF16),
+            pltpu.VMEM((2,) + tile, F32), pltpu.VMEM(tile, F32), pltpu.VMEM(tile, F32),
+            pltpu.VMEM(tile, F32), pltpu.VMEM((2,) + tile, F32),
             pltpu.VMEM((SEQS, FFN), BF16), pltpu.VMEM((SEQS, TN), BF16), pltpu.VMEM((WSLOTS, WIDTH, TN), BF16),
-            pltpu.VMEM((NT, SEQS, TN), F32), pltpu.VMEM((NT, SEQS, TN), F32),
-            dma((WSLOTS,)), dma((NT,)), dma((NT,))],
-        compiler_params=pltpu.CompilerParams(collective_id=2, has_side_effects=True, vmem_limit_bytes=VMEM_ALL),
-        cost_estimate=pl.CostEstimate(flops=2 * 10**10, bytes_accessed=90 * 2**20, transcendentals=0),
-    )(h2, w_gate, w_up, w_down)
+            dma((5,)), dma, dma((2, SLABS)), dma((SLABS,)), dma((SLABS,)), dma((KVSLOTS,)), dma((KVSLOTS,)),
+            dma((2,)), dma((WSLOTS,)), dma, dma((NT,)),
+            dma((CHUNKS,)), dma((CHUNKS,)), dma((CHUNKS,)), dma((CHUNKS,)), dma((CHUNKS,)), dma((CHUNKS,)),
+            dma((NT,)), dma((NT,))],
+        compiler_params=pltpu.CompilerParams(collective_id=0, has_side_effects=True, vmem_limit_bytes=VMEM_ALL),
+        cost_estimate=pl.CostEstimate(flops=3 * 10**10, bytes_accessed=190 * 2**20, transcendentals=0),
+    )(positions, cos_t, sin_t, gain1, gain2, resid_in, w_query, w_key, w_value, k_rows, v_rows, w_out,
+      w_gate, w_up, w_down)
 
 
 def final_kernel(z_ref, zr_ref, x1_ref, out_ref, tb, send_sem, recv_sem):
@@ -566,9 +559,8 @@
         cos_t, sin_t = rope_tables(positions, HD)
         k_rows = k_cache.reshape(SEQS, SLOTS * KVH, HD)
         v_rows = v_cache.reshape(SEQS, SLOTS * KVH, HD)
-        x1, h2, kn, vn = attention(positions, cos_t, sin_t, gain_attn.reshape(32, 128), gain_mlp.reshape(32, 128),
-                                   resid_in, w_query, w_key, w_value, k_rows, v_rows, w_out)
-        z = mlp(h2, w_gate, w_up, w_down)
+        x1, z, kn, vn = layer(positions, cos_t, sin_t, gain_attn.reshape(32, 128), gain_mlp.reshape(32, 128),
+                              resid_in, w_query, w_key, w_value, k_rows, v_rows, w_out, w_gate, w_up, w_down)
         z_peer = lax.ppermute(z, 'tp', [(0, 2), (1, 3), (2, 0), (3, 1)])
         k_full, v_full = write_caches(positions, kn, vn, k_cache, v_cache, z)
         resid_out = finish(z, z_peer, x1)

time: 165 us -> 157 us (0.952)
  Pallas kernels: 158 us -> 150 us
    pallas_call x2 -> x1, Pallas kernels: 108 us -> 100 us  [layer(): pl.pallas_call(layer_kernel, name='layer', out_shape=(shape((SEQS, WIDTH)...]
  transfers between devices with their start and end apart: 1 -> 1, of which waited for: 1 -> 1; matrix products, arithmetic and copies ran while one was open for 0% -> 0% of each run, Pallas kernels for 28% -> 29%
where the time goes in v3:
time: 157 us
  Pallas kernels  150 us (96%)
  waiting for transfers between devices  2.38 us (2%)
  other arithmetic  1.94 us (1%)
    pallas_call x1, Pallas kernels, layer(): pl.pallas_call(layer_kernel, name='layer', out_shape=(shape((SEQS, WIDTH)...  100 us
    pallas_call x1, Pallas kernels, write_caches(): pl.pallas_call(cache_kernel, name='write_caches', out_shape=(cache, cache...  45.9 us
    pallas_call x1, Pallas kernels, finish(): pl.pallas_call(final_kernel, name='finish', out_shape=jax.ShapeDtypeStruc...  4.35 us
  transfers between devices with their start and end apart: 1, of which 1 were waited for; matrix products, arithmetic and copies ran while one was open for 0% of the time, Pallas kernels for 29%

profile of v3, /device:TPU:0, one launch (start us, length us, event | category | flops | bytes accessed | tf_op | source)
XLA Modules:
  0.0 156.6 jit_solution(9091224604705279822)
XLA Ops:
  0.7 0.7 convert_element_type.11
  1.3 1.2 fusion
  2.6 100.0 %layer.1 = (bf16[256,4096]{1,0:T(8,128)(2,1)}, f32[4,256,512]{2,1,0:T(8,128)}, f32[2,256,128]{2,1,0:T(8,128)}, f32[2,256,128]{2,1,0:T(8,128)}) custom-call(s32[256]{0:T(256)} %pos_ref.1, f32[256,128]{1,0:T(8,128)} %get-tuple-element.16.cos_hbm, f32[256,128]{1,0:T(8,128)} %get-tuple-element.15.sin_hbm, bf16[32,128]{1,0:T(8,128)(2,1)} %bitcast.6, ...), custom_call_target="tpu_custom_call" | custom-call | flops 30000001024 | bytes 199229440 | tf_op jit(solution)/shard_map/layer/pallas_call | solution.py:483
  102.6 0.0 collective-permute-start
  102.6 0.0 copy-start
  102.6 0.0 copy-start.1
  102.7 45.9 %write_caches.1 = (bf16[256,256,2,128]{3,2,1,0:T(2,128)(2,1)}, bf16[256,256,2,128]{3,2,1,0:T(2,128)(2,1)}) custom-call(s32[256]{0:T(256)} %pos_ref.1, f32[2,256,128]{2,1,0:T(8,128)} %get-tuple-element.11.kn_ref, f32[2,256,128]{2,1,0:T(8,128)} %get-tuple-element.12.vn_ref, bf16[256,256,2,128]{3,2,1,0:T(2,128)(2,1)} %k_hbm.1, ...), custom_call_target="tpu_custom_call" | custom-call | flops 20000000000 | bytes 134217728 | tf_op jit(solution)/shard_map/write_caches/pallas_call | solution.py:100
  148.5 2.4 %collective-permute-done.zr_ref = f32[4,256,512]{2,1,0:T(8,128)S(1)} collective-permute-done((f32[4,256,512]{2,1,0:T(8,128)}, f32[4,256,512]{2,1,0:T(8,128)S(1)}, u32[]{:S(2)}, u32[]{:S(2)}) %collective-permute-start) | collective-permute-done | bytes 2097184 | tf_op jit(solution)/shard_map/ppermute | solution.py:564
  150.9 0.0 copy-done
  150.9 0.0 copy-done.1
  150.9 4.4 %finish.1 = bf16[256,4096]{1,0:T(8,128)(2,1)S(1)} custom-call(f32[4,256,512]{2,1,0:T(8,128)S(1)} %copy-done.1, f32[4,256,512]{2,1,0:T(8,128)S(1)} %collective-permute-done.zr_ref, bf16[256,4096]{1,0:T(8,128)(2,1)S(1)} %copy-done), custom_call_target="tpu_custom_call" | custom-call | flops 200000000 | bytes 10485760 | tf_op jit(solution)/shard_map/finish/pallas_call | solution.py:543
  155.3 1.3 copy.17
  (1 shorter events, 0.0 us)
Async XLA Ops:
  102.6 48.3 %collective-permute-start = (f32[4,256,512]{2,1,0:T(8,128)}, f32[4,256,512]{2,1,0:T(8,128)S(1)}, u32[]{:S(2)}, u32[]{:S(2)}) collective-permute-start(f32[4,256,512]{2,1,0:T(8,128)} %get-tuple-element.9.z_ref.after_hbm), channel_id=1, source_target_pairs={{0,2},{1,3},{2,0},{3,1},{4,6},{5,7},{6,4},{7,5}} | collective-permute-start | bytes 6291464 | tf_op jit(solution)/shard_map/ppermute | solution.py:564
  102.6 48.3 %copy-start = (bf16[256,4096]{1,0:T(8,128)(2,1)S(1)}, bf16[256,4096]{1,0:T(8,128)(2,1)}, u32[]{:S(2)}) copy-start(bf16[256,4096]{1,0:T(8,128)(2,1)} %get-tuple-element.10.x1_ref) | copy-start | bytes 6291460
  102.6 48.3 %copy-start.1 = (f32[4,256,512]{2,1,0:T(8,128)S(1)}, f32[4,256,512]{2,1,0:T(8,128)}, u32[]{:S(2)}) copy-start(f32[4,256,512]{2,1,0:T(8,128)} %get-tuple-element.9.z_ref.after_hbm) | copy-start | bytes 6291460

commit v4 on v3

--- a/solution.py
+++ b/solution.py
@@ -36,6 +36,10 @@
 WSLOTS = 5
 GT = FFN // TN
 N_TILES = 2 * GT + 2 * NT
+PIECE = 64
+PIECES = NT * SEQS // PIECE
+PER = SEQS // PIECE
+EARLY = 2
 
 
 def rope_tables(positions, head_dim):
@@ -122,11 +126,11 @@
 
 
 def layer_kernel(pos_hbm, cos_hbm, sin_hbm, gain1_hbm, gain2_hbm, x_hbm, wq_hbm, wk_hbm, wv_hbm, k_hbm, v_hbm,
-                 wo_hbm, wg_hbm, wu_hbm, wd_hbm, x1_hbm, z_hbm, kn_ref, vn_ref,
+                 wo_hbm, wg_hbm, wu_hbm, wd_hbm, x1_hbm, zt_ref, z_hbm, kn_ref, vn_ref,
                  pos_ref, cos_ref, sin_ref, gain1_ref, gain2_ref, x_ref, x1_ref, h2, q_ref, gain_row,
                  kbuf, vbuf, wo, o3, o2, ybuf, rb1, sb, rb2, tb, act, gbuf, wbuf,
                  small_sem, x_sem, q_sem, k_sem, v_sem, kc_sem, vc_sem, wo_sem, w_sem, x1_sem, z_sem,
-                 s1, r1, s2, r2, s3, r3, s4, r4):
+                 s1, r1, s2, r2, s3, r3, s4, r4, s5, r5):
     tp = lax.axis_index("tp")
     mine = lax.rem(tp, 2)
     other = 1 - mine
@@ -148,7 +152,7 @@
                 pltpu.make_async_copy(wk_hbm.at[rows], wbuf.at[2, rows, pl.ds(0, kv)], k_sem.at[i]),
                 pltpu.make_async_copy(wv_hbm.at[rows], wbuf.at[2, rows, pl.ds(kv, kv)], v_sem.at[i]))
 
-    for i in range(SLABS):
+    for i in range(2):
         for copy in load_w(i):
             copy.start()
 
@@ -158,15 +162,7 @@
         return (pltpu.make_async_copy(k_hbm.at[seqs], kbuf.at[slot], kc_sem.at[slot]),
                 pltpu.make_async_copy(v_hbm.at[seqs], vbuf.at[slot], vc_sem.at[slot]))
 
-    for g in range(2):
-        for copy in load_kv(g):
-            copy.start()
     load_wo = [pltpu.make_async_copy(wo_hbm.at[:, pl.ds(i * HALF, HALF)], wo.at[i], wo_sem.at[i]) for i in range(2)]
-    for copy in load_wo:
-        copy.start()
-    for g in range(2, KVSLOTS):
-        for copy in load_kv(g):
-            copy.start()
 
     barrier = pltpu.get_barrier_semaphore()
     for device in (partner, peer):
@@ -178,6 +174,9 @@
         copy.wait()
     spread_gain(gain1_ref, gain_row)
     load_x.wait()
+    for i in range(2, SLABS):
+        for copy in load_w(i):
+            copy.start()
 
     def norm_step(i, _):
         rows = pl.ds(pl.multiple_of(i * 16, 16), 16)
@@ -199,6 +198,17 @@
         rows = pl.ds(pl.multiple_of(i * KS, KS), KS)
         for n in range(QKV // TN):
             ybuf[0, n] += jnp.dot(h2[:, rows], wbuf[n, rows, :], preferred_element_type=F32)
+
+        @pl.when(i < KVSLOTS)
+        def _():
+            for copy in load_kv(i):
+                copy.start()
+
+        @pl.when(i == KVSLOTS)
+        def _():
+            for copy in load_wo:
+                copy.start()
+
         return 0
 
     lax.fori_loop(0, SLABS, slab, 0)
@@ -254,11 +264,9 @@
         return pltpu.make_async_copy(wu_hbm.at[:, cols], wbuf.at[slot], w_sem.at[slot])
 
     def load_down(t, slot):
-        if isinstance(t, int):
-            t = jnp.int32(t)
-        far = (t < NT).astype(jnp.int32)
-        half = far * other + (1 - far) * mine
-        start = half * HALF + (t - (1 - far) * NT) * TN
+        near = lax.rem(t, 2)
+        half = near * mine + (1 - near) * other
+        start = half * HALF + (t // 2) * TN
         cols = pl.ds(pl.multiple_of(start, TN), TN)
         return pltpu.make_async_copy(wd_hbm.at[:, cols], wbuf.at[slot, pl.ds(0, FFN)], w_sem.at[slot])
 
@@ -389,6 +397,30 @@
     stage2(CHUNKS - 1)
     stage4(CHUNKS - 4)
 
+    def gate_rows(t, rows):
+        slot = lax.rem(2 * t, WSLOTS)
+        for n in range(TN // 256):
+            gbuf[rows, n * 256:(n + 1) * 256] = jnp.dot(h2[rows, :], wbuf[slot, :, n * 256:(n + 1) * 256],
+                                                        preferred_element_type=F32).astype(BF16)
+
+    def up_rows(t, rows):
+        slot = lax.rem(2 * t + 1, WSLOTS)
+        for n in range(TN // 256):
+            up = jnp.dot(h2[rows, :], wbuf[slot, :, n * 256:(n + 1) * 256],
+                         preferred_element_type=F32).astype(BF16).astype(F32)
+            gate = gbuf[rows, n * 256:(n + 1) * 256].astype(F32)
+            cols = pl.ds(pl.multiple_of(t * TN + n * 256, 256), 256)
+            act[rows, cols] = (jax.nn.silu(gate) * up).astype(BF16)
+
+    def gate_up_early(t, _):
+        load_gate(t, lax.rem(2 * t, WSLOTS)).wait()
+        gate_rows(t, slice(0, SEQS // 2))
+        load_up(t, lax.rem(2 * t + 1, WSLOTS)).wait()
+        up_rows(t, slice(0, SEQS // 2))
+        return 0
+
+    lax.fori_loop(0, EARLY, gate_up_early, 0)
+
     def tail(c, _):
         @pl.when(c < CHUNKS)
         def _():
@@ -416,61 +448,80 @@
     def mm(lhs_ref, slot, depth, n):
         return jnp.dot(lhs_ref[...], wbuf[slot, 0:depth, n * 256:(n + 1) * 256], preferred_element_type=F32)
 
+    def gate_up_late(t, _):
+        gate_rows(t, slice(SEQS // 2, SEQS))
+        start_tile(2 * t + WSLOTS)
+        up_rows(t, slice(SEQS // 2, SEQS))
+        start_tile(2 * t + 1 + WSLOTS)
+        return 0
+
+    lax.fori_loop(0, EARLY, gate_up_late, 0)
+
     def gate_up(t, _):
-        slot = lax.rem(2 * t, WSLOTS)
-        load_gate(t, slot).wait()
-        for n in range(TN // 256):
-            gbuf[:, n * 256:(n + 1) * 256] = mm(h2, slot, WIDTH, n).astype(BF16)
+        load_gate(t, lax.rem(2 * t, WSLOTS)).wait()
+        gate_rows(t, slice(0, SEQS))
         start_tile(2 * t + WSLOTS)
-        slot = lax.rem(2 * t + 1, WSLOTS)
-        load_up(t, slot).wait()
-        for n in range(TN // 256):
-            up = mm(h2, slot, WIDTH, n).astype(BF16).astype(F32)
-            gate = gbuf[:, n * 256:(n + 1) * 256].astype(F32)
-            act[:, pl.ds(pl.multiple_of(t * TN + n * 256, 256), 256)] = (jax.nn.silu(gate) * up).astype(BF16)
+        load_up(t, lax.rem(2 * t + 1, WSLOTS)).wait()
+        up_rows(t, slice(0, SEQS))
         start_tile(2 * t + 1 + WSLOTS)
         return 0
 
-    lax.fori_loop(0, GT, gate_up, 0)
+    lax.fori_loop(EARLY, GT, gate_up, 0)
 
     def send4(t):
         return remote(ybuf.at[other, t], rb1.at[t], s4.at[t], r4.at[t], partner)
 
-    def save_z(t):
-        return pltpu.make_async_copy(sb.at[t], z_hbm.at[t], z_sem.at[t])
-
-    def down_far(t, _):
-        i = 2 * GT + t
+    def save_z(t, j):
+        return pltpu.make_async_copy(sb.at[t, pl.ds(j * PIECE, PIECE)], z_hbm.at[t * PER + j - 1], z_sem.at[t, j])
+
+    send5 = remote(sb.at[0, pl.ds(0, PIECE)], rb2.at[0, pl.ds(0, PIECE)], s5, r5, peer)
+
+    def down(t, _):
+        i = 2 * GT + 2 * t
         slot = lax.rem(i, WSLOTS)
-        load_down(t, slot).wait()
+        load_down(2 * t, slot).wait()
         for n in range(TN // 256):
             ybuf[other, t, :, n * 256:(n + 1) * 256] = mm(act, slot, FFN, n)
         send4(t).start()
         start_tile(i + WSLOTS)
-        return 0
-
-    lax.fori_loop(0, NT, down_far, 0)
-
-    def down_near(t, _):
-        i = 2 * GT + NT + t
-        slot = lax.rem(i, WSLOTS)
-        load_down(NT + t, slot).wait()
+        slot = lax.rem(i + 1, WSLOTS)
+        load_down(2 * t + 1, slot).wait()
+        for n in range(TN // 256):
+            sb[t, :, n * 256:(n + 1) * 256] = mm(act, slot, FFN, n)
+        start_tile(i + 1 + WSLOTS)
         send4(t).wait_recv()
-        for n in range(TN // 256):
-            sb[t, :, n * 256:(n + 1) * 256] = mm(act, slot, FFN, n) + rb1[t, :, n * 256:(n + 1) * 256]
-        save_z(t).start()
-        start_tile(i + WSLOTS)
-        return 0
-
-    lax.fori_loop(0, NT, down_near, 0)
+        sb[t] += rb1[t]
+
+        @pl.when(t == 0)
+        def _():
+            send5.start()
+
+        @pl.when(t > 0)
+        def _():
+            save_z(t, 0).start()
+
+        for j in range(1, PER):
+            save_z(t, j).start()
+        return 0
+
+    lax.fori_loop(0, NT, down, 0)
 
     def sent4(t, _):
         send4(t).wait_send()
-        save_z(t).wait()
+
+        @pl.when(t > 0)
+        def _():
+            save_z(t, 0).wait()
+
+        for j in range(1, PER):
+            save_z(t, j).wait()
         return 0
 
     lax.fori_loop(0, NT, sent4, 0)
     save_x1.wait()
+    send5.wait_send()
+    send5.wait_recv()
+    zt_ref[...] = sb[0, 0:PIECE] + rb2[0, 0:PIECE]
 
 
 def layer(positions, cos_t, sin_t, gain1, gain2, resid_in, w_query, w_key, w_value, k_rows, v_rows, w_out,
@@ -483,10 +534,10 @@
     return pl.pallas_call(
         layer_kernel,
         name="layer",
-        out_shape=(shape((SEQS, WIDTH), BF16), shape(tile, F32),
+        out_shape=(shape((SEQS, WIDTH), BF16), shape((PIECE, TN), F32), shape((PIECES - 1, PIECE, TN), F32),
                    shape((KVH, SEQS, HD), F32), shape((KVH, SEQS, HD), F32)),
         in_specs=[hbm] * 15,
-        out_specs=(hbm, hbm, vmem, vmem),
+        out_specs=(hbm, vmem, hbm, vmem, vmem),
         scratch_shapes=[
             pltpu.SMEM((SEQS,), jnp.int32), pltpu.VMEM((SEQS, HD), F32), pltpu.VMEM((SEQS, HD), F32),
             pltpu.VMEM((32, 128), BF16), pltpu.VMEM((32, 128), BF16),
@@ -499,16 +550,16 @@
             pltpu.VMEM(tile, F32), pltpu.VMEM((2,) + tile, F32),
             pltpu.VMEM((SEQS, FFN), BF16), pltpu.VMEM((SEQS, TN), BF16), pltpu.VMEM((WSLOTS, WIDTH, TN), BF16),
             dma((5,)), dma, dma((2, SLABS)), dma((SLABS,)), dma((SLABS,)), dma((KVSLOTS,)), dma((KVSLOTS,)),
-            dma((2,)), dma((WSLOTS,)), dma, dma((NT,)),
+            dma((2,)), dma((WSLOTS,)), dma, dma((NT, PER)),
             dma((CHUNKS,)), dma((CHUNKS,)), dma((CHUNKS,)), dma((CHUNKS,)), dma((CHUNKS,)), dma((CHUNKS,)),
-            dma((NT,)), dma((NT,))],
+            dma((NT,)), dma((NT,)), dma, dma],
         compiler_params=pltpu.CompilerParams(collective_id=0, has_side_effects=True, vmem_limit_bytes=VMEM_ALL),
         cost_estimate=pl.CostEstimate(flops=3 * 10**10, bytes_accessed=190 * 2**20, transcendentals=0),
     )(positions, cos_t, sin_t, gain1, gain2, resid_in, w_query, w_key, w_value, k_rows, v_rows, w_out,
       w_gate, w_up, w_down)
 
 
-def final_kernel(z_ref, zr_ref, x1_ref, out_ref, tb, send_sem, recv_sem):
+def final_kernel(zt_ref, z_ref, zr_ref, x1_ref, out_ref, tb, send_sem, recv_sem):
     tp = lax.axis_index("tp")
     mine = lax.rem(tp, 2)
     other = 1 - mine
@@ -527,7 +578,9 @@
         out_ref[:, cols] = (x1_ref[:, cols].astype(F32) + tb[half, t]).astype(BF16)
 
     for t in range(NT):
-        tb[mine, t] = z_ref[t] + zr_ref[t]
+        for j in range(PER):
+            p = t * PER + j - 1
+            tb[mine, t, j * PIECE:(j + 1) * PIECE] = zt_ref[...] if p < 0 else z_ref[p] + zr_ref[p]
         copy(mine, t).start()
     for t in range(NT):
         add(mine, t)
@@ -538,19 +591,19 @@
         copy(mine, t).wait_send()
 
 
-def finish(z, z_peer, x1):
+def finish(z_first, z, z_peer, x1):
     vmem = pl.BlockSpec(memory_space=pltpu.VMEM)
     return pl.pallas_call(
         final_kernel,
         name="finish",
         out_shape=jax.ShapeDtypeStruct((SEQS, WIDTH), BF16),
-        in_specs=[vmem] * 3,
+        in_specs=[vmem] * 4,
         out_specs=vmem,
         scratch_shapes=[pltpu.VMEM((2, NT, SEQS, TN), F32), pltpu.SemaphoreType.DMA((NT,)),
                         pltpu.SemaphoreType.DMA((NT,))],
         compiler_params=pltpu.CompilerParams(collective_id=1, has_side_effects=True, vmem_limit_bytes=24 * 2**20),
         cost_estimate=pl.CostEstimate(flops=2 * 10**8, bytes_accessed=10 * 2**20, transcendentals=0),
-    )(z, z_peer, x1)
+    )(z_first, z, z_peer, x1)
 
 
 def solution(mesh):
@@ -559,11 +612,11 @@
         cos_t, sin_t = rope_tables(positions, HD)
         k_rows = k_cache.reshape(SEQS, SLOTS * KVH, HD)
         v_rows = v_cache.reshape(SEQS, SLOTS * KVH, HD)
-        x1, z, kn, vn = layer(positions, cos_t, sin_t, gain_attn.reshape(32, 128), gain_mlp.reshape(32, 128),
+        x1, z_first, z, kn, vn = layer(positions, cos_t, sin_t, gain_attn.reshape(32, 128), gain_mlp.reshape(32, 128),
                               resid_in, w_query, w_key, w_value, k_rows, v_rows, w_out, w_gate, w_up, w_down)
         z_peer = lax.ppermute(z, 'tp', [(0, 2), (1, 3), (2, 0), (3, 1)])
         k_full, v_full = write_caches(positions, kn, vn, k_cache, v_cache, z)
-        resid_out = finish(z, z_peer, x1)
+        resid_out = finish(z_first, z, z_peer, x1)
         return resid_out, k_full, v_full
 
     row_spec = P('dp', None)

time: 157 us -> 150 us (0.955)
  Pallas kernels: 150 us -> 146 us
  waiting for transfers between devices: 2.38 us -> 0.01 us
    pallas_call x1, Pallas kernels: 100 us -> 95.3 us  [layer(): pl.pallas_call(layer_kernel, name='layer', out_shape=(shape((SEQS, WIDTH)...]
    ppermute x1, waiting for transfers between devices: 2.38 us -> 0.01 us  [layer_local(): z_peer = lax.ppermute(z, 'tp', [(0, 2), (1, 3), (2, 0), (3, 1)])]
  transfers between devices with their start and end apart: 1 -> 1, of which waited for: 1 -> 0; matrix products, arithmetic and copies ran while one was open for 0% -> 0% of each run, Pallas kernels for 29% -> 31%
where the time goes in v4:
time: 150 us
  Pallas kernels  146 us (97%)
  other arithmetic  1.94 us (1%)
    pallas_call x1, Pallas kernels, layer(): pl.pallas_call(layer_kernel, name='layer', out_shape=(shape((SEQS, WIDTH)...  95.3 us
    pallas_call x1, Pallas kernels, write_caches(): pl.pallas_call(cache_kernel, name='write_caches', out_shape=(cache, cache...  45.9 us
    pallas_call x1, Pallas kernels, finish(): pl.pallas_call(final_kernel, name='finish', out_shape=jax.ShapeDtypeStruc...  4.67 us
  transfers between devices with their start and end apart: 1, of which 0 were waited for; matrix products, arithmetic and copies ran while one was open for 0% of the time, Pallas kernels for 31%

profile of v4, /device:TPU:0, one launch (start us, length us, event | category | flops | bytes accessed | tf_op | source)
XLA Modules:
  0.0 149.8 jit_solution(859865215223306897)
XLA Ops:
  0.7 0.7 convert_element_type.11
  1.3 1.2 fusion
  2.6 95.3 %layer.1 = (bf16[256,4096]{1,0:T(8,128)(2,1)}, f32[64,512]{1,0:T(8,128)}, f32[15,64,512]{2,1,0:T(8,128)}, f32[2,256,128]{2,1,0:T(8,128)}, f32[2,256,128]{2,1,0:T(8,128)}) custom-call(s32[256]{0:T(256)} %pos_ref.1, f32[256,128]{1,0:T(8,128)} %get-tuple-element.18.cos_hbm, f32[256,128]{1,0:T(8,128)} %get-tuple-element.17.sin_hbm, bf16[32,128]{1,0:T(8,128)(2,1)} %bitcast.6, ...), custom_call_target="tpu_custom_call" | custom-call | flops 30000001024 | bytes 199229440 | tf_op jit(solution)/shard_map/layer/pallas_call | solution.py:534
  97.8 0.0 collective-permute-start
  97.9 0.0 copy-start
  97.9 0.0 copy-start.1
  97.9 0.0 copy-start.2
  97.9 45.9 %write_caches.1 = (bf16[256,256,2,128]{3,2,1,0:T(2,128)(2,1)}, bf16[256,256,2,128]{3,2,1,0:T(2,128)(2,1)}) custom-call(s32[256]{0:T(256)} %pos_ref.1, f32[2,256,128]{2,1,0:T(8,128)} %get-tuple-element.13.kn_ref, f32[2,256,128]{2,1,0:T(8,128)} %get-tuple-element.14.vn_ref, bf16[256,256,2,128]{3,2,1,0:T(2,128)(2,1)} %k_hbm.1, ...), custom_call_target="tpu_custom_call" | custom-call | flops 20000000000 | bytes 134217728 | tf_op jit(solution)/shard_map/write_caches/pallas_call | solution.py:104
  143.8 0.0 collective-permute-done.zr_ref
  143.8 0.0 copy-done
  143.8 0.0 copy-done.1
  143.8 0.0 copy-done.2
  143.8 4.7 %finish.1 = bf16[256,4096]{1,0:T(8,128)(2,1)S(1)} custom-call(f32[64,512]{1,0:T(8,128)S(1)} %copy-done.2, f32[15,64,512]{2,1,0:T(8,128)S(1)} %copy-done.1, f32[15,64,512]{2,1,0:T(8,128)S(1)} %collective-permute-done.zr_ref, bf16[256,4096]{1,0:T(8,128)(2,1)S(1)} %copy-done), custom_call_target="tpu_custom_call" | custom-call | flops 200000000 | bytes 10485760 | tf_op jit(solution)/shard_map/finish/pallas_call | solution.py:596
  148.5 1.3 copy.17
  (1 shorter events, 0.0 us)
Async XLA Ops:
  97.8 45.9 %collective-permute-start = (f32[15,64,512]{2,1,0:T(8,128)}, f32[15,64,512]{2,1,0:T(8,128)S(1)}, u32[]{:S(2)}, u32[]{:S(2)}) collective-permute-start(f32[15,64,512]{2,1,0:T(8,128)} %get-tuple-element.11.z_ref.after_hbm), channel_id=1, source_target_pairs={{0,2},{1,3},{2,0},{3,1},{4,6},{5,7},{6,4},{7,5}} | collective-permute-start | bytes 5898248 | tf_op jit(solution)/shard_map/ppermute | solution.py:617
  97.9 45.9 %copy-start = (bf16[256,4096]{1,0:T(8,128)(2,1)S(1)}, bf16[256,4096]{1,0:T(8,128)(2,1)}, u32[]{:S(2)}) copy-start(bf16[256,4096]{1,0:T(8,128)(2,1)} %get-tuple-element.12.x1_ref) | copy-start | bytes 6291460
  97.9 45.9 %copy-start.1 = (f32[15,64,512]{2,1,0:T(8,128)S(1)}, f32[15,64,512]{2,1,0:T(8,128)}, u32[]{:S(2)}) copy-start(f32[15,64,512]{2,1,0:T(8,128)} %get-tuple-element.11.z_ref.after_hbm) | copy-start | bytes 5898244
  97.9 45.9 %copy-start.2 = (f32[64,512]{1,0:T(8,128)S(1)}, f32[64,512]{1,0:T(8,128)}, u32[]{:S(2)}) copy-start(f32[64,512]{1,0:T(8,128)} %get-tuple-element.10.zt_ref) | copy-start | bytes 393220

commit v5 on v4

--- a/solution.py
+++ b/solution.py
@@ -2,6 +2,7 @@
 import math
 import jax
 import jax.numpy as jnp
+import numpy as np
 from jax import lax
 from jax.experimental import pallas as pl
 from jax.experimental.pallas import tpu as pltpu
@@ -42,19 +43,20 @@
 EARLY = 2
 
 
-def rope_tables(positions, head_dim):
+def rope_tables(head_dim):
     half_dim = head_dim // 2
-    lane = jnp.arange(head_dim)
-    exponents = (lane % half_dim).astype(jnp.float32) * (2.0 / head_dim)
-    inv_freq = 1.0 / jnp.power(ROPE_THETA, exponents)
+    lane = np.arange(head_dim)
+    inv_freq = 1.0 / ROPE_THETA ** ((lane % half_dim) * (2.0 / head_dim))
     wavelen = (2.0 * math.pi) / inv_freq
     smooth = (ORIG_CTX / wavelen - LOW_FACTOR) / (HIGH_FACTOR - LOW_FACTOR)
     blended = (1.0 - smooth) * inv_freq / ROPE_FACTOR + smooth * inv_freq
-    inv_freq = jnp.where(wavelen < ORIG_CTX / HIGH_FACTOR, inv_freq,
-                         jnp.where(wavelen > ORIG_CTX / LOW_FACTOR, inv_freq / ROPE_FACTOR, blended))
-    angles = positions[:, None].astype(jnp.float32) * inv_freq[None, :]
-    sign = jnp.where(lane < half_dim, -1.0, 1.0).astype(jnp.float32)
-    return jnp.cos(angles), jnp.sin(angles) * sign[None, :]
+    inv_freq = np.where(wavelen < ORIG_CTX / HIGH_FACTOR, inv_freq,
+                        np.where(wavelen > ORIG_CTX / LOW_FACTOR, inv_freq / ROPE_FACTOR, blended))
+    angles = np.arange(SLOTS, dtype=np.float32)[:, None] * inv_freq.astype(np.float32)[None, :]
+    angles = angles.astype(np.float64)
+    sign = np.where(lane < half_dim, -1.0, 1.0)
+    shape = (SLOTS, 1, head_dim)
+    return (np.cos(angles).astype(np.float32).reshape(shape), (np.sin(angles) * sign).astype(np.float32).reshape(shape))
 
 
 CBLK = 8
@@ -127,7 +129,7 @@
 
 def layer_kernel(pos_hbm, cos_hbm, sin_hbm, gain1_hbm, gain2_hbm, x_hbm, wq_hbm, wk_hbm, wv_hbm, k_hbm, v_hbm,
                  wo_hbm, wg_hbm, wu_hbm, wd_hbm, x1_hbm, zt_ref, z_hbm, kn_ref, vn_ref,
-                 pos_ref, cos_ref, sin_ref, gain1_ref, gain2_ref, x_ref, x1_ref, h2, q_ref, gain_row,
+                 pos_ref, cos_tab, sin_tab, cos_ref, sin_ref, gain1_ref, gain2_ref, x_ref, x1_ref, h2, q_ref, gain_row,
                  kbuf, vbuf, wo, o3, o2, ybuf, rb1, sb, rb2, tb, act, gbuf, wbuf,
                  small_sem, x_sem, q_sem, k_sem, v_sem, kc_sem, vc_sem, wo_sem, w_sem, x1_sem, z_sem,
                  s1, r1, s2, r2, s3, r3, s4, r4, s5, r5):
@@ -140,7 +142,7 @@
     load_x = pltpu.make_async_copy(x_hbm, x_ref, x_sem)
     load_x.start()
     small = [pltpu.make_async_copy(src, dst, small_sem.at[i]) for i, (src, dst) in enumerate(
-        ((gain1_hbm, gain1_ref), (gain2_hbm, gain2_ref), (cos_hbm, cos_ref), (sin_hbm, sin_ref), (pos_hbm, pos_ref)))]
+        ((gain1_hbm, gain1_ref), (gain2_hbm, gain2_ref), (cos_hbm, cos_tab), (sin_hbm, sin_tab), (pos_hbm, pos_ref)))]
     for copy in small:
         copy.start()
 
@@ -173,8 +175,18 @@
     for copy in small:
         copy.wait()
     spread_gain(gain1_ref, gain_row)
+
+    def pick(i, _):
+        for j in range(8):
+            row = i * 8 + j
+            pos = pos_ref[row]
+            cos_ref[pl.ds(row, 1), :] = cos_tab[pos]
+            sin_ref[pl.ds(row, 1), :] = sin_tab[pos]
+        return 0
+
+    lax.fori_loop(0, SEQS // 8, pick, 0)
     load_x.wait()
-    for i in range(2, SLABS):
+    for i in range(2, SLABS - 2):
         for copy in load_w(i):
             copy.start()
 
@@ -198,6 +210,11 @@
         rows = pl.ds(pl.multiple_of(i * KS, KS), KS)
         for n in range(QKV // TN):
             ybuf[0, n] += jnp.dot(h2[:, rows], wbuf[n, rows, :], preferred_element_type=F32)
+
+        @pl.when(i < 2)
+        def _():
+            for copy in load_w(i + SLABS - 2):
+                copy.start()
 
         @pl.when(i < KVSLOTS)
         def _():
@@ -539,7 +556,8 @@
         in_specs=[hbm] * 15,
         out_specs=(hbm, vmem, hbm, vmem, vmem),
         scratch_shapes=[
-            pltpu.SMEM((SEQS,), jnp.int32), pltpu.VMEM((SEQS, HD), F32), pltpu.VMEM((SEQS, HD), F32),
+            pltpu.SMEM((SEQS,), jnp.int32), pltpu.VMEM((SLOTS, 1, HD), F32), pltpu.VMEM((SLOTS, 1, HD), F32),
+            pltpu.VMEM((SEQS, HD), F32), pltpu.VMEM((SEQS, HD), F32),
             pltpu.VMEM((32, 128), BF16), pltpu.VMEM((32, 128), BF16),
             pltpu.VMEM((SEQS, WIDTH), BF16), pltpu.VMEM((SEQS, WIDTH), BF16), pltpu.VMEM((SEQS, WIDTH), BF16),
             pltpu.VMEM((QH * PITCH, HD), F32), pltpu.VMEM((8, WIDTH), F32),
@@ -609,7 +627,7 @@
 def solution(mesh):
     def layer_local(resid_in, positions, k_cache, v_cache, gain_attn, w_query, w_key, w_value,
                     w_out, gain_mlp, w_gate, w_up, w_down):
-        cos_t, sin_t = rope_tables(positions, HD)
+        cos_t, sin_t = (jnp.asarray(table) for table in rope_tables(HD))
         k_rows = k_cache.reshape(SEQS, SLOTS * KVH, HD)
         v_rows = v_cache.reshape(SEQS, SLOTS * KVH, HD)
         x1, z_first, z, kn, vn = layer(positions, cos_t, sin_t, gain_attn.reshape(32, 128), gain_mlp.reshape(32, 128),

time: 150 us -> 148 us (0.987)
  other arithmetic: 1.94 us -> 0 us
where the time goes in v5:
time: 148 us
  Pallas kernels  146 us (99%)
    pallas_call x1, Pallas kernels, layer(): pl.pallas_call(layer_kernel, name='layer', out_shape=(shape((SEQS, WIDTH)...  95.4 us
    pallas_call x1, Pallas kernels, write_caches(): pl.pallas_call(cache_kernel, name='write_caches', out_shape=(cache, cache...  45.9 us
    pallas_call x1, Pallas kernels, finish(): pl.pallas_call(final_kernel, name='finish', out_shape=jax.ShapeDtypeStruc...  4.69 us
  transfers between devices with their start and end apart: 1, of which 0 were waited for; matrix products, arithmetic and copies ran while one was open for 0% of the time, Pallas kernels for 31%

profile of v5, /device:TPU:0, one launch (start us, length us, event | category | flops | bytes accessed | tf_op | source)
XLA Modules:
  0.0 148.1 jit_solution(5280927664934016080)
XLA Ops:
  0.6 95.4 %layer.1 = (bf16[256,4096]{1,0:T(8,128)(2,1)}, f32[64,512]{1,0:T(8,128)}, f32[15,64,512]{2,1,0:T(8,128)}, f32[2,256,128]{2,1,0:T(8,128)}, f32[2,256,128]{2,1,0:T(8,128)}) custom-call(s32[256]{0:T(256)} %pos_ref.1, f32[256,1,128]{2,1,0:T(1,128)} %constant.4.clone.cos_hbm, f32[256,1,128]{2,1,0:T(1,128)} %constant.5.clone.sin_hbm, bf16[32,128]{1,0:T(8,128)(2,1)} %bitcast.6, ...), custom_call_target="tpu_custom_call" | custom-call | flops 30000001024 | bytes 199229440 | tf_op jit(solution)/shard_map/layer/pallas_call | solution.py:551
  96.1 0.0 collective-permute-start
  96.1 0.0 copy-start
  96.1 0.0 copy-start.1
  96.1 0.0 copy-start.2
  96.1 45.9 %write_caches.1 = (bf16[256,256,2,128]{3,2,1,0:T(2,128)(2,1)}, bf16[256,256,2,128]{3,2,1,0:T(2,128)(2,1)}) custom-call(s32[256]{0:T(256)} %pos_ref.1, f32[2,256,128]{2,1,0:T(8,128)} %get-tuple-element.13.kn_ref, f32[2,256,128]{2,1,0:T(8,128)} %get-tuple-element.14.vn_ref, bf16[256,256,2,128]{3,2,1,0:T(2,128)(2,1)} %k_hbm.1, ...), custom_call_target="tpu_custom_call" | custom-call | flops 20000000000 | bytes 134217728 | tf_op jit(solution)/shard_map/write_caches/pallas_call | solution.py:106
  142.0 0.0 collective-permute-done.zr_ref
  142.0 0.0 copy-done
  142.0 0.0 copy-done.1
  142.0 0.0 copy-done.2
  142.1 4.7 %finish.1 = bf16[256,4096]{1,0:T(8,128)(2,1)S(1)} custom-call(f32[64,512]{1,0:T(8,128)S(1)} %copy-done.2, f32[15,64,512]{2,1,0:T(8,128)S(1)} %copy-done.1, f32[15,64,512]{2,1,0:T(8,128)S(1)} %collective-permute-done.zr_ref, bf16[256,4096]{1,0:T(8,128)(2,1)S(1)} %copy-done), custom_call_target="tpu_custom_call" | custom-call | flops 200000000 | bytes 10485760 | tf_op jit(solution)/shard_map/finish/pallas_call | solution.py:614
  146.8 1.3 copy.19
Async XLA Ops:
  96.1 45.9 %collective-permute-start = (f32[15,64,512]{2,1,0:T(8,128)}, f32[15,64,512]{2,1,0:T(8,128)S(1)}, u32[]{:S(2)}, u32[]{:S(2)}) collective-permute-start(f32[15,64,512]{2,1,0:T(8,128)} %get-tuple-element.11.z_ref.after_hbm), channel_id=1, source_target_pairs={{0,2},{1,3},{2,0},{3,1},{4,6},{5,7},{6,4},{7,5}} | collective-permute-start | bytes 5898248 | tf_op jit(solution)/shard_map/ppermute | solution.py:635
  96.1 45.9 %copy-start = (bf16[256,4096]{1,0:T(8,128)(2,1)S(1)}, bf16[256,4096]{1,0:T(8,128)(2,1)}, u32[]{:S(2)}) copy-start(bf16[256,4096]{1,0:T(8,128)(2,1)} %get-tuple-element.12.x1_ref) | copy-start | bytes 6291460
  96.1 45.9 %copy-start.1 = (f32[15,64,512]{2,1,0:T(8,128)S(1)}, f32[15,64,512]{2,1,0:T(8,128)}, u32[]{:S(2)}) copy-start(f32[15,64,512]{2,1,0:T(8,128)} %get-tuple-element.11.z_ref.after_hbm) | copy-start | bytes 5898244
  96.1 45.9 %copy-start.2 = (f32[64,512]{1,0:T(8,128)S(1)}, f32[64,512]{1,0:T(8,128)}, u32[]{:S(2)}) copy-start(f32[64,512]{1,0:T(8,128)} %get-tuple-element.10.zt_ref) | copy-start | bytes 393220
